TPU v7x, 256 devices: a whole 4x4x8 slice. The times are simulated.
256 devices in a mesh: dp: 8 (over y, core), expert: 8 (over z), ffn: 4 (over x).
Axes of the slice: x: 4, y: 4, z: 8, core: 2. Of those that a mesh axis runs over, the one named last changes fastest.
Arguments:
- tokens: bfloat16 [1024, 4096], P('expert'), may hold values from -6 to 6
- expert_ids: int32 [1024, 2], P('expert'), may hold values from 0 to 7, all different within a row; in each aligned block of 128 rows (0 to 127, 128 to 255, ...) at most 64 rows name the same one
- route_weight: float32 [1024, 2], P('expert'), may hold values from 0.05 to 1
- cotangent: bfloat16 [1024, 4096], P('expert'), may hold values from -40 to 40
- w_gate: bfloat16 [8, 7168, 4096], P('expert', ('dp', 'ffn')), may hold values from -0.09375 to 0.09375
- w_up: bfloat16 [8, 7168, 4096], P('expert', ('dp', 'ffn')), may hold values from -0.09375 to 0.09375
- w_down: bfloat16 [8, 7168, 4096], P('expert', ('dp', 'ffn')), may hold values from -0.0625 to 0.0625
Outputs:
- layer_out: bfloat16 [1024, 4096], P('expert', ('dp', 'ffn'))
- ascent_gate: bfloat16 [8, 7168, 4096], P('expert', ('dp', 'ffn'))
- ascent_up: bfloat16 [8, 7168, 4096], P('expert', ('dp', 'ffn'))
- ascent_down: bfloat16 [8, 7168, 4096], P('expert', ('dp', 'ffn'))
Inputs may be any that keep to these rules, and one draw needn't show every extreme that they name: `expert_ids`: each row names two different experts. Among the rows of one aligned block of 128 no expert is named more than 64 times; in every draw some block names some expert exactly 64 times.
All inputs are finite; a program needn't handle non-finite values.
Results may differ from a plain program's by a relative error of at most 0.017.
Values may be sent and summed in bfloat16 or wider, within the bound.
A program may use at most 128 MiB of HBM per device.

v0:
```python
import functools

import jax
import jax.numpy as jnp
from jax import lax
from jax.sharding import Mesh
from jax.sharding import PartitionSpec as P

FF = 7168
DP_FFN = ("dp_0", "dp_1", "ffn")
DP_EXPERT_FFN = ("dp_0", "dp_1", "expert", "ffn")


def sent_together(arrays, axis, split_dim, concat_dim, along):
    widths = [a.shape[along] for a in arrays]
    both = jnp.concatenate(arrays, axis=along)
    whole = lax.all_to_all(both, axis, split_axis=split_dim, concat_axis=concat_dim, tiled=True)
    return tuple(jnp.split(whole, [sum(widths[:k]) for k in range(1, len(widths))], axis=along))


def side_by_side(arrays, axis, dim, along):
    both = jnp.concatenate(arrays, axis=along)
    whole, at, gathered = (lax.all_gather(both, axis, axis=dim, tiled=True), 0, [])
    for a in arrays:
        gathered.append(lax.slice_in_dim(whole, at, at + a.shape[along], axis=along))
        at += a.shape[along]
    return tuple(gathered)


def by_axis(x, axes):
    return functools.reduce(lax.psum, axes, x)


def split_up(x, dim, devices):
    lengths = x.shape
    tiles = x.reshape(*lengths[:dim], devices, lengths[dim] // devices, *lengths[dim + 1 :])
    return jnp.moveaxis(tiles, dim, 0)


def sum_at_owner(x, axis, dim):
    devices = lax.axis_size(axis)
    tiles = lax.all_to_all(split_up(x, dim, devices), axis, 0, 0, tiled=True)
    return jnp.sum(tiles.astype(jnp.float32), axis=0)


def silu_parts(pre_act):
    sigmoid_value = jax.nn.sigmoid(pre_act)
    return (pre_act * sigmoid_value, sigmoid_value * (1.0 + pre_act * (1.0 - sigmoid_value)))


def against_rows(left_rows, right_rows):
    return lax.dot_general(
        left_rows, right_rows, (((0,), (0,)), ((), ())), preferred_element_type=jnp.float32
    )


def across_width(left_rows, weight):
    return lax.dot_general(
        left_rows, weight, (((1,), (1,)), ((), ())), preferred_element_type=jnp.float32
    )


def squares_of(matrix):
    return jnp.sum(matrix * matrix)


def on_device(tokens, expert_ids, route_weight, cotangent, w_gate, w_up, w_down):
    tok_rows, feature_width = tokens.shape
    experts = lax.axis_size("expert")
    groups = lax.axis_size(DP_FFN)
    capacity = tok_rows // 2
    slot_count = experts * capacity
    column_width = feature_width // groups
    chosen = expert_ids[:, :, None] == jnp.arange(experts, dtype=jnp.int32)[None, None, :]
    per_token = jnp.sum(chosen.astype(jnp.int32), axis=1)
    earlier = jnp.cumsum(per_token, axis=0) - per_token
    position = jnp.sum(jnp.where(chosen, earlier[:, None, :], 0), axis=2)
    slot_index = expert_ids * capacity + position
    slot_hot = slot_index[:, :, None] == jnp.arange(slot_count, dtype=jnp.int32)[None, None, :]
    hot_all = slot_hot.reshape(tok_rows * 2, slot_count).astype(jnp.bfloat16)
    scaled = (route_weight[:, :, None] * cotangent.astype(jnp.float32)[:, None, :]).astype(
        jnp.bfloat16
    )
    token_slots = against_rows(hot_all, jnp.repeat(tokens, 2, axis=0)).astype(jnp.bfloat16)
    grad_slots = against_rows(hot_all, scaled.reshape(tok_rows * 2, feature_width)).astype(
        jnp.bfloat16
    )
    token_cube = token_slots.reshape(experts, capacity, feature_width)
    grad_cube = grad_slots.reshape(experts, capacity, feature_width)
    column_start = lax.axis_index(DP_FFN) * column_width
    token_part = lax.dynamic_slice_in_dim(token_cube, column_start, column_width, 2)
    grad_part = lax.dynamic_slice_in_dim(grad_cube, column_start, column_width, 2)
    received = sent_together((token_part, grad_part), "expert", 0, 0, 1)
    slot_rows, slot_grads = side_by_side(
        (
            received[0].reshape(slot_count, column_width),
            received[1].reshape(slot_count, column_width),
        ),
        DP_FFN,
        1,
        0,
    )
    gate_weight = w_gate[0]
    up_weight = w_up[0]
    down_weight = w_down[0]
    pre_gate = across_width(slot_rows, gate_weight)
    pre_up = across_width(slot_rows, up_weight)
    activated, derivative = silu_parts(pre_gate)
    hidden = (activated * pre_up).astype(jnp.bfloat16)
    partial_value = jnp.dot(hidden, down_weight, preferred_element_type=jnp.float32)
    grad_down = against_rows(hidden, slot_grads)
    grad_hidden = across_width(slot_grads, down_weight)
    delta_gate = (grad_hidden * pre_up * derivative).astype(jnp.bfloat16)
    delta_up = (grad_hidden * activated).astype(jnp.bfloat16)
    grad_gate = against_rows(delta_gate, slot_rows)
    grad_up = against_rows(delta_up, slot_rows)
    sum_squares = by_axis(
        squares_of(grad_gate) + squares_of(grad_up) + squares_of(grad_down), DP_EXPERT_FFN
    )
    summed = sum_at_owner(partial_value.astype(jnp.bfloat16), DP_FFN, 1).astype(jnp.bfloat16)
    summed = summed.reshape(experts, capacity, column_width)
    returned_rows = lax.all_to_all(
        summed, "expert", split_axis=0, concat_axis=0, tiled=True
    ).reshape(slot_count, column_width)
    picked = jnp.dot(hot_all, returned_rows, preferred_element_type=jnp.float32).reshape(
        tok_rows, 2, column_width
    )
    layer_out = jnp.sum(route_weight[:, :, None] * picked, axis=1).astype(jnp.bfloat16)
    inv_rms = lax.rsqrt(sum_squares / (3.0 * experts * FF * feature_width) + 1e-06)
    return (
        layer_out,
        (grad_gate * inv_rms).astype(jnp.bfloat16)[None],
        (grad_up * inv_rms).astype(jnp.bfloat16)[None],
        (grad_down * inv_rms).astype(jnp.bfloat16)[None],
    )


def solution(mesh):
    finer = Mesh(
        mesh.devices.reshape(4, 2, mesh.shape["expert"], mesh.shape["ffn"]),
        ("dp_0", "dp_1", "expert", "ffn"),
    )
    placed = (
        P("expert", None),
        P("expert", None),
        P("expert", None),
        P("expert", None),
        P("expert", DP_FFN, None),
        P("expert", DP_FFN, None),
        P("expert", DP_FFN, None),
    )
    return jax.shard_map(
        on_device,
        mesh=finer,
        in_specs=placed,
        out_specs=(
            P("expert", DP_FFN),
            P("expert", DP_FFN, None),
            P("expert", DP_FFN, None),
            P("expert", DP_FFN, None),
        ),
        check_vma=False,
    )
```

profile of v0, /device:TPU:2, one launch (start us, length us, event | category | flops | bytes accessed | tf_op | source)
XLA Modules:
  0.0 226.5 jit_solution(17055700325028920306)
XLA Ops:
  9.8 2.8 %convert_element_type.44 = f32[128,4096]{1,0:T(8,128)} convert(bf16[128,4096]{1,0:T(8,128)(2,1)} %param.10) | non-fusion elementwise | flops 524288 | bytes 3145728 | tf_op jit(solution)/shard_map/convert_element_type | solution.py:81
  12.6 1.3 bitcast_convert_fusion.1
  14.2 1.4 bitcast_convert_fusion
  15.7 20.1 %all_to_all.15 = bf16[8,128,128]{2,1,0:T(8,128)(2,1)S(1)} all-to-all(bf16[8,128,128]{2,1,0:T(8,128)(2,1)S(1)} %pad_maximum_fusion), channel_id=1, replica_groups=mesh['dp_0'=4,'dp_1'=2,'expert'=8,'ffn'=4] {'expert'}, dimensions={0} | all-to-all | bytes 524288 | tf_op jit(solution)/shard_map/all_to_all | solution.py:17
  36.6 60.0 %all-gather.2.cloned.1.call-done = bf16[1024,4096]{1,0:T(8,128)(2,1)} async-done(((bf16[1024,128]{1,0:T(8,128)(2,1)}), bf16[1024,4096]{1,0:T(8,128)(2,1)}) %all-gather.2.cloned.1.call-update) | async-done | bytes 8388624 | tf_op jit(solution)/shard_map/all_gather | solution.py:23
  96.6 4.3 %fusion.10 = f32[512,224]{0,1:T(8,128)S(1)} fusion(bf16[1024,4096]{1,0:T(8,128)(2,1)} %all-gather.2.cloned.1.call-done, bf16[1,224,4096]{2,1,0:T(8,128)(2,1)} %param.11), kind=kOutput, calls=%fused_computation.21 | convolution fusion | flops 939524096 | bytes 6488064 | tf_op jit(solution)/shard_map/dot_general | solution.py:58
  101.8 2.9 %multiply_convert_fusion.7 = (bf16[512,224]{0,1:T(8,128)(2,1)S(1)}, f32[512,224]{0,1:T(8,128)S(1)}) fusion(f32[512,224]{0,1:T(8,128)S(1)} %fusion.10, bf16[1,224,4096]{2,1,0:T(8,128)(2,1)} %param.12, bf16[1024,4096]{1,0:T(8,128)(2,1)S(1)} %copy-done.5), kind=kOutput, calls=%fused_computation.41 | convolution fusion | flops 940212224 | bytes 7176192 | tf_op jit(solution)/shard_map/dot_general | solution.py:58
  104.7 1.3 fusion.12
  106.0 3.1 %copy.20 = bf16[64,32,8,128]{3,2,0,1:T(8,128)(2,1)} copy(bf16[64,32,8,128]{3,2,1,0:T(8,128)(2,1)S(1)} %fusion.12) | data formatting | bytes 8388608 | tf_op jit(solution)/shard_map/reshape | solution.py:36
  109.1 6.3 %all-to-all-start.1 = ((bf16[32,512,128]{2,1,0:T(8,128)(2,1)}), bf16[32,512,128]{2,1,0:T(8,128)(2,1)}, u32[]{:S(2)}, u32[]{:S(2)}) async-start(bf16[32,512,128]{2,1,0:T(8,128)(2,1)} %bitcast.45), calls=%async_computation.1 | async-start | bytes 8388608 | tf_op jit(solution)/shard_map/all_to_all | solution.py:42
  115.4 3.8 %fusion.2 = f32[512,224]{0,1:T(8,128)S(1)} fusion(bf16[1024,4096]{1,0:T(8,128)(2,1)} %all-gather.2.cloned.1.call-done, bf16[1,224,4096]{2,1,0:T(8,128)(2,1)S(1)} %copy-done), kind=kOutput, calls=%fused_computation.7 | convolution fusion | flops 939524096 | bytes 6488064 | tf_op jit(solution)/shard_map/dot_general | solution.py:58
  119.2 5.9 %multiply_reduce_fusion.1 = (f32[]{:T(128)}, f32[224,4096]{1,0:T(8,128)}) fusion(bf16[1024,4096]{1,0:T(8,128)(2,1)} %all-gather.2.cloned.1.call-done, f32[512,224]{0,1:T(8,128)S(1)} %fusion.2, f32[512,224]{0,1:T(8,128)S(1)} %fusion.10), kind=kOutput, calls=%fused_computation.13 | convolution fusion | flops 942047232 | bytes 8781828 | tf_op jit(solution)/shard_map/dot_general | solution.py:52
  125.2 3.7 %multiply_reduce_fusion.2 = (f32[]{:T(128)}, f32[224,4096]{1,0:T(8,128)}) fusion(bf16[1024,4096]{1,0:T(8,128)(2,1)S(1)} %bitcast.52, f32[512,224]{0,1:T(8,128)S(1)} %fusion.10, f32[512,224]{0,1:T(8,128)S(1)} %fusion.2, f32[512,224]{0,1:T(8,128)S(1)} %get-tuple-element.7), kind=kOutput, calls=%fused_computation.14 | convolution fusion | flops 942505984 | bytes 9240580 | tf_op jit(solution)/shard_map/dot_general | solution.py:52
  130.2 5.8 %multiply_reduce_fusion = (f32[]{:T(128)}, f32[224,4096]{1,0:T(8,128)}) fusion(bf16[512,224]{0,1:T(8,128)(2,1)S(1)} %get-tuple-element.6, bf16[1024,4096]{1,0:T(8,128)(2,1)} %all-gather.2.cloned.1.call-done), kind=kOutput, calls=%fused_computation.12 | convolution fusion | flops 941359104 | bytes 8093700 | tf_op jit(solution)/shard_map/dot_general | solution.py:52
  136.7 29.0 %psum.28 = f32[]{:T(128)} all-reduce(f32[]{:T(128)S(6)} %add.43), channel_id=1, replica_groups=mesh['dp_0'=4,'dp_1'=2,'expert'=8,'ffn'=4] {'dp_0'}, use_global_device_ids=true, to_apply=%region_8.9 | all-reduce | flops 1 | bytes 8 | tf_op jit(solution)/shard_map/psum | solution.py:31
  165.7 3.1 %psum.29 = f32[]{:T(128)} all-reduce(f32[]{:T(128)} %psum.28), channel_id=1, replica_groups=mesh['dp_0'=4,'dp_1'=2,'expert'=8,'ffn'=4] {'dp_1'}, use_global_device_ids=true, to_apply=%region_9.10 | all-reduce | flops 1 | bytes 8 | tf_op jit(solution)/shard_map/psum | solution.py:31
  168.8 18.1 %psum.30 = f32[]{:T(128)} all-reduce(f32[]{:T(128)} %psum.29), channel_id=1, replica_groups=mesh['dp_0'=4,'dp_1'=2,'expert'=8,'ffn'=4] {'expert'}, use_global_device_ids=true, to_apply=%region_10.11 | all-reduce | flops 1 | bytes 8 | tf_op jit(solution)/shard_map/psum | solution.py:31
  186.8 9.1 %psum.31 = f32[]{:T(128)} all-reduce(f32[]{:T(128)} %psum.30), channel_id=1, replica_groups=mesh['dp_0'=4,'dp_1'=2,'expert'=8,'ffn'=4] {'ffn'}, use_global_device_ids=true, to_apply=%region_11.12 | all-reduce | flops 1 | bytes 8 | tf_op jit(solution)/shard_map/psum | solution.py:31
  196.6 3.7 %fusion.15 = bf16[1,224,4096]{2,1,0:T(8,128)(2,1)} fusion(f32[224,4096]{1,0:T(8,128)} %get-tuple-element.9, f32[]{:T(128)S(6)} %rsqrt.3), kind=kLoop, calls=%fused_computation.26 | loop fusion | flops 1835008 | bytes 5505028 | tf_op jit(solution)/shard_map/broadcast_in_dim | solution.py:132
  200.3 1.5 fusion.17
  201.8 3.5 %reduce_sum.68 = bf16[512,128]{1,0:T(8,128)(2,1)} reduce(bf16[32,512,128]{2,1,0:T(8,128)(2,1)} %all-to-all-done.1, bf16[]{:T(256)} %constant.36.clone.1), dimensions={0}, to_apply=%region_3.4 | reduce | flops 2031616 | bytes 4325378 | tf_op jit(solution)/shard_map/reduce_sum | solution.py:43
  205.3 4.4 %all-to-all-start.2 = ((bf16[8,64,128]{2,1,0:T(8,128)(2,1)}), bf16[8,64,128]{2,1,0:T(8,128)(2,1)S(1)}, u32[]{:S(2)}, u32[]{:S(2)}) async-start(bf16[8,64,128]{2,1,0:T(8,128)(2,1)} %bitcast.11), calls=%async_computation.2 | async-start | bytes 262144 | tf_op jit(solution)/shard_map/all_to_all | solution.py:122
  209.6 3.5 %fusion.16 = bf16[1,224,4096]{2,1,0:T(8,128)(2,1)} fusion(f32[224,4096]{1,0:T(8,128)} %get-tuple-element.11, f32[]{:T(128)S(6)} %rsqrt.3), kind=kLoop, calls=%fused_computation.27 | loop fusion | flops 1835008 | bytes 5505028 | tf_op jit(solution)/shard_map/broadcast_in_dim | solution.py:133
  213.2 5.5 %all-to-all-done.2 = bf16[8,64,128]{2,1,0:T(8,128)(2,1)S(1)} async-done(((bf16[8,64,128]{2,1,0:T(8,128)(2,1)}), bf16[8,64,128]{2,1,0:T(8,128)(2,1)S(1)}, u32[]{:S(2)}, u32[]{:S(2)}) %all-to-all-start.2) | async-done | bytes 131104 | tf_op jit(solution)/shard_map/all_to_all | solution.py:122
  (32 shorter events, 5.6 us)
Async XLA Ops:
  7.2 97.6 %copy-start = (bf16[1,224,4096]{2,1,0:T(8,128)(2,1)S(1)}, bf16[1,224,4096]{2,1,0:T(8,128)(2,1)}, u32[]{:S(2)}) copy-start(bf16[1,224,4096]{2,1,0:T(8,128)(2,1)} %param.13) | copy-start | bytes 5505028
  7.2 5.5 %copy-start.3 = (bf16[128,4096]{1,0:T(8,128)(2,1)S(1)}, bf16[128,4096]{1,0:T(8,128)(2,1)}, u32[]{:S(2)}) copy-start(bf16[128,4096]{1,0:T(8,128)(2,1)} %param.7) | copy-start | bytes 3145732
  7.2 89.4 %all-gather.2.cloned.1.call-start = ((), (), s32[]{:S(2)}) async-start(), calls=%async_computation.3 | async-start | bytes 8650752 | tf_op jit(solution)/shard_map/all_gather | solution.py:23
  12.6 1.6 copy-start.1
  12.6 1.6 copy-start.4
  96.6 5.2 %copy-start.5 = (bf16[1024,4096]{1,0:T(8,128)(2,1)S(1)}, bf16[1024,4096]{1,0:T(8,128)(2,1)}, u32[]{:S(2)}) copy-start(bf16[1024,4096]{1,0:T(8,128)(2,1)} %all-gather.2.cloned.1.call-done) | copy-start | bytes 25165828
  109.1 92.7 %all-to-all-start.1 = ((bf16[32,512,128]{2,1,0:T(8,128)(2,1)}), bf16[32,512,128]{2,1,0:T(8,128)(2,1)}, u32[]{:S(2)}, u32[]{:S(2)}) async-start(bf16[32,512,128]{2,1,0:T(8,128)(2,1)} %bitcast.45), calls=%async_computation.1 | async-start | bytes 8388608 | tf_op jit(solution)/shard_map/all_to_all | solution.py:42
  115.4 9.7 %slice-start = ((s8[8388608]{0:T(1024)(128)(4,1)}), s8[4194304]{0:T(1024)(128)(4,1)S(1)}, s32[]{:S(2)}) async-start(s8[8388608]{0:T(1024)(128)(4,1)} %bitcast.51), calls=%async_computation.4 | async-start | bytes 8388608
  119.2 5.9 %slice-start.1 = ((s8[8388608]{0:T(1024)(128)(4,1)}), s8[4194304]{0:T(1024)(128)(4,1)S(1)}, s32[]{:S(2)}) async-start(s8[8388608]{0:T(1024)(128)(4,1)} %bitcast.51), calls=%async_computation.5 | async-start | bytes 8388608
  196.6 3.7 %copy-start.2 = (f32[224,4096]{1,0:T(8,128)S(1)}, f32[224,4096]{1,0:T(8,128)}, u32[]{:S(2)}) copy-start(f32[224,4096]{1,0:T(8,128)} %get-tuple-element.13) | copy-start | bytes 11010052
  205.3 13.4 %all-to-all-start.2 = ((bf16[8,64,128]{2,1,0:T(8,128)(2,1)}), bf16[8,64,128]{2,1,0:T(8,128)(2,1)S(1)}, u32[]{:S(2)}, u32[]{:S(2)}) async-start(bf16[8,64,128]{2,1,0:T(8,128)(2,1)} %bitcast.11), calls=%async_computation.2 | async-start | bytes 262144 | tf_op jit(solution)/shard_map/all_to_all | solution.py:122
Sparse Core Ops, SparseCore 0:
  36.8 59.8 all-gather.1
where the time goes:
time: 228 us; the launch traced here: 226 us
  blocking collectives  79.4 us (35%)
  waiting for transfers between devices  65.5 us (29%)
  matrix products  31.3 us (14%)
  other arithmetic  18.2 us (8%)
  between operations  16.8 us (7%)
  starting transfers between devices  10.7 us (5%)
  local copies, waits for them, and re-layouts  4.55 us (2%)
    all_gather x1, waiting for transfers between devices, side_by_side(): lax.all_gather(both, axis, axis=dim, tiled=True)  60 us
    psum x4, blocking collectives, by_axis(): return functools.reduce(lax.psum, axes, x)  59.2 us
    all_to_all x1, blocking collectives, sent_together(): lax.all_to_all(both, axis, split_axis=split_dim, concat_axis=concat_dim,...  20.1 us
    dot_general x5, matrix products, against_rows(): lax.dot_general(left_rows, right_rows, (((0,), (0,)), ((), ())), preferre...  18.1 us
    dot_general x3, matrix products, across_width(): lax.dot_general(left_rows, weight, (((1,), (1,)), ((), ())), preferred_el...  11 us
    all_to_all x1, starting transfers between devices, sum_at_owner(): tiles = lax.all_to_all(split_up(x, dim, devices), axis, 0, 0, tiled=True)  6.28 us
    all_to_all x1, waiting for transfers between devices, on_device(): lax.all_to_all(summed, 'expert', split_axis=0, concat_axis=0, tiled=True)  5.53 us
  transfers between devices with their start and end apart: 3, of which 2 were waited for; matrix products, arithmetic and copies ran while one was open for 12% of the time, Pallas kernels for 0%

commit v1 on v0

--- a/solution.py
+++ b/solution.py
@@ -1,5 +1,3 @@
-import functools
-
 import jax
 import jax.numpy as jnp
 from jax import lax
@@ -25,10 +23,6 @@
         gathered.append(lax.slice_in_dim(whole, at, at + a.shape[along], axis=along))
         at += a.shape[along]
     return tuple(gathered)
-
-
-def by_axis(x, axes):
-    return functools.reduce(lax.psum, axes, x)
 
 
 def split_up(x, dim, devices):
@@ -114,7 +108,7 @@
     delta_up = (grad_hidden * activated).astype(jnp.bfloat16)
     grad_gate = against_rows(delta_gate, slot_rows)
     grad_up = against_rows(delta_up, slot_rows)
-    sum_squares = by_axis(
+    sum_squares = lax.psum(
         squares_of(grad_gate) + squares_of(grad_up) + squares_of(grad_down), DP_EXPERT_FFN
     )
     summed = sum_at_owner(partial_value.astype(jnp.bfloat16), DP_FFN, 1).astype(jnp.bfloat16)

time: 228 us -> 265 us (1.16)
  blocking collectives: 79.4 us -> 115 us
    psum x4 -> x1, blocking collectives: 59.2 us -> 95.2 us  [on_device(): lax.psum(squares_of(grad_gate) + squares_of(grad_up) + squares_of(grad_do...]
  transfers between devices with their start and end apart: 3 -> 3, of which waited for: 2 -> 2; matrix products, arithmetic and copies ran while one was open for 12% -> 11% of each run, Pallas kernels for 0% -> 0%
where the time goes in v1:
time: 265 us; the launch traced here: 263 us
  blocking collectives  115 us (43%)
  waiting for transfers between devices  65.6 us (25%)
  matrix products  31.3 us (12%)
  other arithmetic  18.2 us (7%)
  between operations  16.8 us (6%)
  starting transfers between devices  11.2 us (4%)
  local copies, waits for them, and re-layouts  4.55 us (2%)
    psum x1, blocking collectives, on_device(): lax.psum(squares_of(grad_gate) + squares_of(grad_up) + squares_of(grad_do...  95.2 us
    all_gather x1, waiting for transfers between devices, side_by_side(): lax.all_gather(both, axis, axis=dim, tiled=True)  60 us
    all_to_all x1, blocking collectives, sent_together(): lax.all_to_all(both, axis, split_axis=split_dim, concat_axis=concat_dim,...  20.1 us
    dot_general x5, matrix products, against_rows(): lax.dot_general(left_rows, right_rows, (((0,), (0,)), ((), ())), preferre...  18.1 us
    dot_general x3, matrix products, across_width(): lax.dot_general(left_rows, weight, (((1,), (1,)), ((), ())), preferred_el...  11 us
    all_to_all x1, starting transfers between devices, sum_at_owner(): tiles = lax.all_to_all(split_up(x, dim, devices), axis, 0, 0, tiled=True)  6.28 us
    all_to_all x1, waiting for transfers between devices, on_device(): lax.all_to_all(summed, 'expert', split_axis=0, concat_axis=0, tiled=True)  5.57 us
  transfers between devices with their start and end apart: 3, of which 2 were waited for; matrix products, arithmetic and copies ran while one was open for 11% of the time, Pallas kernels for 0%

profile of v1, /device:TPU:2, one launch (start us, length us, event | category | flops | bytes accessed | tf_op | source)
XLA Modules:
  0.0 263.0 jit_solution(3693468779245802273)
XLA Ops:
  7.2 0.9 convert_reduce_fusion
  9.8 2.8 %convert_element_type.44 = f32[128,4096]{1,0:T(8,128)} convert(bf16[128,4096]{1,0:T(8,128)(2,1)} %param.10) | non-fusion elementwise | flops 524288 | bytes 3145728 | tf_op jit(solution)/shard_map/convert_element_type | solution.py:75
  12.6 1.3 bitcast_convert_fusion.1
  14.2 1.4 bitcast_convert_fusion
  15.7 20.1 %all_to_all.15 = bf16[8,128,128]{2,1,0:T(8,128)(2,1)S(1)} all-to-all(bf16[8,128,128]{2,1,0:T(8,128)(2,1)S(1)} %pad_maximum_fusion), channel_id=1, replica_groups=mesh['dp_0'=4,'dp_1'=2,'expert'=8,'ffn'=4] {'expert'}, dimensions={0} | all-to-all | bytes 524288 | tf_op jit(solution)/shard_map/all_to_all | solution.py:15
  36.6 60.0 %all-gather.2.cloned.1.call-done = bf16[1024,4096]{1,0:T(8,128)(2,1)} async-done(((bf16[1024,128]{1,0:T(8,128)(2,1)}), bf16[1024,4096]{1,0:T(8,128)(2,1)}) %all-gather.2.cloned.1.call-update) | async-done | bytes 8388624 | tf_op jit(solution)/shard_map/all_gather | solution.py:21
  96.6 4.3 %fusion.10 = f32[512,224]{0,1:T(8,128)S(1)} fusion(bf16[1024,4096]{1,0:T(8,128)(2,1)} %all-gather.2.cloned.1.call-done, bf16[1,224,4096]{2,1,0:T(8,128)(2,1)} %param.11), kind=kOutput, calls=%fused_computation.21 | convolution fusion | flops 939524096 | bytes 6488064 | tf_op jit(solution)/shard_map/dot_general | solution.py:52
  100.9 0.8 copy-done.5
  101.8 2.9 %multiply_convert_fusion.7 = (bf16[512,224]{0,1:T(8,128)(2,1)S(1)}, f32[512,224]{0,1:T(8,128)S(1)}) fusion(f32[512,224]{0,1:T(8,128)S(1)} %fusion.10, bf16[1,224,4096]{2,1,0:T(8,128)(2,1)} %param.12, bf16[1024,4096]{1,0:T(8,128)(2,1)S(1)} %copy-done.5), kind=kOutput, calls=%fused_computation.41 | convolution fusion | flops 940212224 | bytes 7176192 | tf_op jit(solution)/shard_map/dot_general | solution.py:52
  104.7 1.3 fusion.12
  106.0 3.1 %copy.20 = bf16[64,32,8,128]{3,2,0,1:T(8,128)(2,1)} copy(bf16[64,32,8,128]{3,2,1,0:T(8,128)(2,1)S(1)} %fusion.12) | data formatting | bytes 8388608 | tf_op jit(solution)/shard_map/reshape | solution.py:30
  109.1 6.3 %all-to-all-start.1 = ((bf16[32,512,128]{2,1,0:T(8,128)(2,1)}), bf16[32,512,128]{2,1,0:T(8,128)(2,1)}, u32[]{:S(2)}, u32[]{:S(2)}) async-start(bf16[32,512,128]{2,1,0:T(8,128)(2,1)} %bitcast.45), calls=%async_computation.1 | async-start | bytes 8388608 | tf_op jit(solution)/shard_map/all_to_all | solution.py:36
  115.4 3.8 %fusion.2 = f32[512,224]{0,1:T(8,128)S(1)} fusion(bf16[1024,4096]{1,0:T(8,128)(2,1)} %all-gather.2.cloned.1.call-done, bf16[1,224,4096]{2,1,0:T(8,128)(2,1)S(1)} %copy-done), kind=kOutput, calls=%fused_computation.7 | convolution fusion | flops 939524096 | bytes 6488064 | tf_op jit(solution)/shard_map/dot_general | solution.py:52
  119.2 5.9 %multiply_reduce_fusion.1 = (f32[]{:T(128)}, f32[224,4096]{1,0:T(8,128)}) fusion(bf16[1024,4096]{1,0:T(8,128)(2,1)} %all-gather.2.cloned.1.call-done, f32[512,224]{0,1:T(8,128)S(1)} %fusion.2, f32[512,224]{0,1:T(8,128)S(1)} %fusion.10), kind=kOutput, calls=%fused_computation.13 | convolution fusion | flops 942047232 | bytes 8781828 | tf_op jit(solution)/shard_map/dot_general | solution.py:46
  125.2 3.7 %multiply_reduce_fusion.2 = (f32[]{:T(128)}, f32[224,4096]{1,0:T(8,128)}) fusion(bf16[1024,4096]{1,0:T(8,128)(2,1)S(1)} %bitcast.52, f32[512,224]{0,1:T(8,128)S(1)} %fusion.10, f32[512,224]{0,1:T(8,128)S(1)} %fusion.2, f32[512,224]{0,1:T(8,128)S(1)} %get-tuple-element.7), kind=kOutput, calls=%fused_computation.14 | convolution fusion | flops 942505984 | bytes 9240580 | tf_op jit(solution)/shard_map/dot_general | solution.py:46
  130.2 5.8 %multiply_reduce_fusion = (f32[]{:T(128)}, f32[224,4096]{1,0:T(8,128)}) fusion(bf16[512,224]{0,1:T(8,128)(2,1)S(1)} %get-tuple-element.6, bf16[1024,4096]{1,0:T(8,128)(2,1)} %all-gather.2.cloned.1.call-done), kind=kOutput, calls=%fused_computation.12 | convolution fusion | flops 941359104 | bytes 8093700 | tf_op jit(solution)/shard_map/dot_general | solution.py:46
  136.7 95.2 %psum.7 = f32[]{:T(128)} all-reduce(f32[]{:T(128)S(6)} %add.37), channel_id=1, replica_groups=mesh['dp_0'=4,'dp_1'=2,'expert'=8,'ffn'=4] {'dp_0','dp_1','expert','ffn'}, use_global_device_ids=true, to_apply=%region_8.9 | all-reduce | flops 1 | bytes 8 | tf_op jit(solution)/shard_map/psum | solution.py:111
  232.6 3.7 %fusion.15 = bf16[1,224,4096]{2,1,0:T(8,128)(2,1)} fusion(f32[224,4096]{1,0:T(8,128)} %get-tuple-element.9, f32[]{:T(128)S(6)} %rsqrt.3), kind=kLoop, calls=%fused_computation.26 | loop fusion | flops 1835008 | bytes 5505028 | tf_op jit(solution)/shard_map/broadcast_in_dim | solution.py:126
  236.3 1.5 fusion.17
  237.8 3.5 %reduce_sum.68 = bf16[512,128]{1,0:T(8,128)(2,1)} reduce(bf16[32,512,128]{2,1,0:T(8,128)(2,1)} %all-to-all-done.1, bf16[]{:T(256)} %constant.36.clone.1), dimensions={0}, to_apply=%region_3.4 | reduce | flops 2031616 | bytes 4325378 | tf_op jit(solution)/shard_map/reduce_sum | solution.py:37
  241.2 4.8 %all-to-all-start.2 = ((bf16[8,64,128]{2,1,0:T(8,128)(2,1)}), bf16[8,64,128]{2,1,0:T(8,128)(2,1)S(1)}, u32[]{:S(2)}, u32[]{:S(2)}) async-start(bf16[8,64,128]{2,1,0:T(8,128)(2,1)} %bitcast.11), calls=%async_computation.2 | async-start | bytes 262144 | tf_op jit(solution)/shard_map/all_to_all | solution.py:116
  246.1 3.5 %fusion.16 = bf16[1,224,4096]{2,1,0:T(8,128)(2,1)} fusion(f32[224,4096]{1,0:T(8,128)} %get-tuple-element.11, f32[]{:T(128)S(6)} %rsqrt.3), kind=kLoop, calls=%fused_computation.27 | loop fusion | flops 1835008 | bytes 5505028 | tf_op jit(solution)/shard_map/broadcast_in_dim | solution.py:127
  249.6 5.6 %all-to-all-done.2 = bf16[8,64,128]{2,1,0:T(8,128)(2,1)S(1)} async-done(((bf16[8,64,128]{2,1,0:T(8,128)(2,1)}), bf16[8,64,128]{2,1,0:T(8,128)(2,1)S(1)}, u32[]{:S(2)}, u32[]{:S(2)}) %all-to-all-start.2) | async-done | bytes 131104 | tf_op jit(solution)/shard_map/all_to_all | solution.py:116
  255.2 0.9 fusion.22
  (29 shorter events, 3.0 us)
Async XLA Ops:
  7.2 97.6 %copy-start = (bf16[1,224,4096]{2,1,0:T(8,128)(2,1)S(1)}, bf16[1,224,4096]{2,1,0:T(8,128)(2,1)}, u32[]{:S(2)}) copy-start(bf16[1,224,4096]{2,1,0:T(8,128)(2,1)} %param.13) | copy-start | bytes 5505028
  7.2 5.5 %copy-start.3 = (bf16[128,4096]{1,0:T(8,128)(2,1)S(1)}, bf16[128,4096]{1,0:T(8,128)(2,1)}, u32[]{:S(2)}) copy-start(bf16[128,4096]{1,0:T(8,128)(2,1)} %param.7) | copy-start | bytes 3145732
  7.2 89.4 %all-gather.2.cloned.1.call-start = ((), (), s32[]{:S(2)}) async-start(), calls=%async_computation.3 | async-start | bytes 8650752 | tf_op jit(solution)/shard_map/all_gather | solution.py:21
  12.6 1.6 copy-start.1
  12.6 1.6 copy-start.4
  96.6 5.2 %copy-start.5 = (bf16[1024,4096]{1,0:T(8,128)(2,1)S(1)}, bf16[1024,4096]{1,0:T(8,128)(2,1)}, u32[]{:S(2)}) copy-start(bf16[1024,4096]{1,0:T(8,128)(2,1)} %all-gather.2.cloned.1.call-done) | copy-start | bytes 25165828
  109.1 128.6 %all-to-all-start.1 = ((bf16[32,512,128]{2,1,0:T(8,128)(2,1)}), bf16[32,512,128]{2,1,0:T(8,128)(2,1)}, u32[]{:S(2)}, u32[]{:S(2)}) async-start(bf16[32,512,128]{2,1,0:T(8,128)(2,1)} %bitcast.45), calls=%async_computation.1 | async-start | bytes 8388608 | tf_op jit(solution)/shard_map/all_to_all | solution.py:36
  115.4 9.7 %slice-start = ((s8[8388608]{0:T(1024)(128)(4,1)}), s8[4194304]{0:T(1024)(128)(4,1)S(1)}, s32[]{:S(2)}) async-start(s8[8388608]{0:T(1024)(128)(4,1)} %bitcast.51), calls=%async_computation.4 | async-start | bytes 8388608
  119.2 5.9 %slice-start.1 = ((s8[8388608]{0:T(1024)(128)(4,1)}), s8[4194304]{0:T(1024)(128)(4,1)S(1)}, s32[]{:S(2)}) async-start(s8[8388608]{0:T(1024)(128)(4,1)} %bitcast.51), calls=%async_computation.5 | async-start | bytes 8388608
  232.5 3.7 %copy-start.2 = (f32[224,4096]{1,0:T(8,128)S(1)}, f32[224,4096]{1,0:T(8,128)}, u32[]{:S(2)}) copy-start(f32[224,4096]{1,0:T(8,128)} %get-tuple-element.13) | copy-start | bytes 11010052
  241.2 14.0 %all-to-all-start.2 = ((bf16[8,64,128]{2,1,0:T(8,128)(2,1)}), bf16[8,64,128]{2,1,0:T(8,128)(2,1)S(1)}, u32[]{:S(2)}, u32[]{:S(2)}) async-start(bf16[8,64,128]{2,1,0:T(8,128)(2,1)} %bitcast.11), calls=%async_computation.2 | async-start | bytes 262144 | tf_op jit(solution)/shard_map/all_to_all | solution.py:116
Sparse Core Ops, SparseCore 0:
  36.8 59.8 all-gather.1

commit v2 on v1

v2 whole, which is shorter than its diff:
```python
import functools

import jax
import jax.numpy as jnp
from jax import lax
from jax.experimental import pallas as pl
from jax.experimental.pallas import tpu as pltpu
from jax.sharding import PartitionSpec as P

MESH = pl.DeviceIdType.MESH
BF = jnp.bfloat16
F32 = jnp.float32
LANES = 128
RING = 4
LEFT, RIGHT, FAR = 3, 1, 2
EVENTS = (
    ((0, 0),),
    ((LEFT, 0), (RIGHT, 0)),
    ((0, LEFT), (0, RIGHT)),
    ((FAR, 0),),
    ((LEFT, LEFT), (LEFT, RIGHT), (RIGHT, LEFT), (RIGHT, RIGHT)),
    ((0, FAR),),
    ((FAR, LEFT), (FAR, RIGHT)),
    ((LEFT, FAR), (RIGHT, FAR), (FAR, FAR)),
)


def dot(a, b, dims):
    return lax.dot_general(a, b, (dims, ((), ())), preferred_element_type=F32)


def body(
    ids, weight, tokens, cotangent, w_gate, w_up, w_down,
    gate_out, up_out, down_out, inv_out, layer_out,
    tok, cot, hot, hot_t, send, slots, w_gu, w_d, acc, hid_t, hid, delta, grads,
    psend, prem, part, relay, joined, half, last, final, back, sq_send, sq_recv,
    local, z_s, z_r, a_s, a_r, b_s, b_r, d_s, d_r, p_s, p_r, q_s, q_r, j_s, j_r,
    l_s, l_r, k_s, k_r, sq_s, sq_r,
    *, experts, total,
):
    dp, z, x = lax.axis_index("dp"), lax.axis_index("expert"), lax.axis_index("ffn")
    y, c = dp // 2, dp % 2
    cap = tok.shape[0] // 2
    count = experts * cap
    units = w_gate.shape[1]
    two, four = count // 2, count // 4

    def at(v, step):
        return (v + step) % RING

    def device(x_=x, y_=y, c_=c, z_=z):
        return {"dp": y_ * 2 + c_, "expert": z_, "ffn": x_}

    def slice_of(x_, y_, c_):
        return (2 * y_ + c_) * RING + x_

    started = []

    def put(src, dst, s_sem, r_sem, dev):
        copy = pltpu.make_async_remote_copy(
            src_ref=src, dst_ref=dst, send_sem=s_sem, recv_sem=r_sem, device_id=dev, device_id_type=MESH
        )
        copy.start()
        started.append(copy)

    def arrived(dst, s_sem, r_sem):
        pltpu.make_async_remote_copy(
            src_ref=dst, dst_ref=dst, send_sem=s_sem, recv_sem=r_sem,
            device_id=device(c_=1 - c), device_id_type=MESH,
        ).wait_recv()

    mine = slice_of(x, y, c)
    columns = pl.ds(pl.multiple_of(mine * LANES, LANES), LANES)
    loads = [
        pltpu.make_async_copy(tokens.at[:, columns], tok, local.at[0]),
        pltpu.make_async_copy(cotangent.at[:, columns], cot, local.at[1]),
        pltpu.make_async_copy(w_gate.at[0], w_gu.at[pl.ds(0, units)], local.at[2]),
        pltpu.make_async_copy(w_up.at[0], w_gu.at[pl.ds(units, units)], local.at[3]),
        pltpu.make_async_copy(w_down.at[0], w_d.at[pl.ds(0, units)], local.at[4]),
    ]
    for load in loads:
        load.start()

    peers = [device(c_=1 - c)]
    peers += [device(x_=at(x, s)) for s in (1, 2, 3)] + [device(y_=at(y, s)) for s in (1, 2, 3)]
    peers += [device(z_=(z + j) % experts) for j in range(1, experts)]
    barrier = pltpu.get_barrier_semaphore()
    for peer in peers:
        pl.semaphore_signal(barrier, inc=1, device_id=peer, device_id_type=MESH)

    rows = tok.shape[0]
    names = lax.broadcasted_iota(jnp.int32, (experts, rows), 0)
    chosen = [names == ids[k : k + 1, :] for k in (0, 1)]
    per_token = (chosen[0].astype(F32) + chosen[1].astype(F32)).astype(BF)
    before = (
        lax.broadcasted_iota(jnp.int32, (rows, rows), 0) < lax.broadcasted_iota(jnp.int32, (rows, rows), 1)
    ).astype(F32).astype(BF)
    earlier = dot(per_token, before, ((1,), (0,)))
    numbers = lax.broadcasted_iota(jnp.int32, (count, rows), 0).astype(F32)
    for k in (0, 1):
        position = jnp.sum(jnp.where(chosen[k], earlier, 0.0), axis=0, keepdims=True)
        slot = ids[k : k + 1, :].astype(F32) * float(cap) + position
        hot[k] = (numbers == slot).astype(F32).astype(BF)

    loads[0].wait()
    loads[1].wait()
    send[0] = dot(hot[0] + hot[1], tok[...], ((1,), (0,))).astype(BF)
    wide = cot[...].astype(F32)
    scaled = [(weight[:, k : k + 1] * wide).astype(BF) for k in (0, 1)]
    send[1] = (
        dot(hot[0], scaled[0], ((1,), (0,))) + dot(hot[1], scaled[1], ((1,), (0,)))
    ).astype(BF)
    own_rows = pl.ds(pl.multiple_of(z * cap, cap), cap)
    pl.semaphore_wait(barrier, len(peers))
    for j in range(1, experts):
        to = (z + j) % experts
        to_rows = pl.ds(pl.multiple_of(to * cap, cap), cap)
        for p in (0, 1):
            put(
                send.at[p, to_rows], slots.at[p, mine, own_rows],
                z_s.at[p, j - 1], z_r.at[p, j - 1], device(z_=to),
            )
    for p in (0, 1):
        slots[p, mine, own_rows, :] = send[p, own_rows, :]
    acc[...] = jnp.zeros_like(acc)
    pad = w_d.shape[0] - units
    if pad:
        w_d[pl.ds(units, pad), :] = jnp.zeros((pad, w_d.shape[1]), BF)
        hid_t[pl.ds(units, pad), :] = jnp.zeros((pad, count), BF)
    for k in (0, 1):
        hot_t[k] = hot[k].astype(F32).T.astype(BF)
    for load in loads[2:]:
        load.wait()
    for j in range(1, experts):
        source = (z + experts - j) % experts
        from_rows = pl.ds(pl.multiple_of(source * cap, cap), cap)
        for p in (0, 1):
            arrived(slots.at[p, mine, from_rows], z_s.at[p, j - 1], z_r.at[p, j - 1])

    def place(p, k, m):
        return (at(x, k), at(y, m)) if p == 0 else (at(x, m), at(y, k))

    def own_slice(p, k, m):
        return slice_of(*place(p, k, m), c)

    def along(p, stage, step):
        return device(x_=at(x, step)) if (p == 0) == (stage == 0) else device(y_=at(y, step))

    def whole(p, s):
        return slots.at[p, s]

    def part_of(p, s, h):
        return slots.at[p, s, pl.ds(h * two, two)]

    def both_ways(p, stage, s, s_sem, r_sem):
        for n, step in ((0, LEFT), (1, RIGHT)):
            put(whole(p, s), whole(p, s), s_sem(n), r_sem(n), along(p, stage, step))

    def onward(p, stage, s, step, s_sem, r_sem):
        n, h, to = (3, 0, RIGHT) if step == LEFT else (2, 1, LEFT)
        ref = part_of(p, s, h)
        put(ref, ref, s_sem(n), r_sem(n), along(p, stage, to))

    def sem_a(p):
        return (lambda n: a_s.at[p, n]), (lambda n: a_r.at[p, n])

    def sem_b(p, k):
        return (lambda n: b_s.at[p, k, n]), (lambda n: b_r.at[p, k, n])

    def await_slice(p, k, m):
        if (k, m) == (0, 0):
            return
        s = own_slice(p, k, m)
        step, (s_sem, r_sem) = (k, sem_a(p)) if m == 0 else (m, sem_b(p, k))
        if step == LEFT:
            arrived(whole(p, s), s_sem(1), r_sem(1))
        elif step == RIGHT:
            arrived(whole(p, s), s_sem(0), r_sem(0))
        else:
            arrived(part_of(p, s, 0), s_sem(3), r_sem(3))
            arrived(part_of(p, s, 1), s_sem(2), r_sem(2))

    def accumulate(p, k, m):
        x_, y_ = place(p, k, m)
        pair = [slice_of(x_, y_, e) for e in (0, 1)]
        cols = [pl.ds(pl.multiple_of(s * LANES, LANES), LANES) for s in pair]
        right = jnp.concatenate([slots[p, s] for s in pair], axis=1)
        if p == 0:
            left = jnp.concatenate([w_gu[:, d] for d in cols], axis=1)
            acc[pl.ds(0, 2 * units), :] += dot(left, right, ((1,), (1,)))
        else:
            left = jnp.concatenate([w_d[pl.ds(0, units), d] for d in cols], axis=1)
            acc[pl.ds(2 * units, units), :] += dot(left, right, ((1,), (1,)))

    def finish(event):
        for k, m in event:
            for p in (0, 1):
                x_, y_ = place(p, k, m)
                arrived(whole(p, slice_of(x_, y_, 1 - c)), d_s.at[p, k, m], d_r.at[p, k, m])
        for k, m in event:
            for p in (0, 1):
                accumulate(p, k, m)

    previous = None
    for event in EVENTS:
        for k, m in event:
            for p in (0, 1):
                await_slice(p, k, m)
                s = own_slice(p, k, m)
                if m == 0:
                    if k == 0:
                        both_ways(p, 0, s, *sem_a(p))
                    elif k != FAR:
                        onward(p, 0, s, k, *sem_a(p))
                elif m != FAR:
                    onward(p, 1, s, m, *sem_b(p, k))
        for k, m in event:
            for p in (0, 1):
                s = own_slice(p, k, m)
                if m == 0:
                    both_ways(p, 1, s, *sem_b(p, k))
                put(whole(p, s), whole(p, s), d_s.at[p, k, m], d_r.at[p, k, m], device(c_=1 - c))
        if previous is not None:
            finish(previous)
        previous = event
    finish(previous)

    block = 32

    def activate(i, carry):
        r = pl.multiple_of(i * block, block)
        gate = acc[pl.ds(r, block), :]
        up = acc[pl.ds(units + r, block), :]
        grad = acc[pl.ds(2 * units + r, block), :]
        s = jax.nn.sigmoid(gate)
        active = gate * s
        hid_t[pl.ds(r, block), :] = (active * up).astype(BF)
        delta[pl.ds(r, block), :] = (grad * up * (s * (1.0 + gate * (1.0 - s)))).astype(BF)
        delta[pl.ds(units + r, block), :] = (grad * active).astype(BF)
        return carry

    lax.fori_loop(0, units // block, activate, 0)
    for i in range(hid_t.shape[0] // LANES):
        r = pl.ds(i * LANES, LANES)
        hid[:, r] = hid_t[r, :].astype(F32).T.astype(BF)

    width = RING * LANES

    def terms(y_, c_):
        cols = pl.ds(pl.multiple_of((2 * y_ + c_) * width, width), width)
        return dot(hid[...], w_d[:, cols], ((1,), (0,)))

    def partner_terms(i, carry):
        t = terms(i, 1 - c)
        for n in range(RING):
            psend[i, n] = t[:, n * LANES : (n + 1) * LANES].astype(BF)
        return carry

    lax.fori_loop(0, RING, partner_terms, 0)
    for i in range(RING):
        put(psend.at[i], prem.at[i], p_s.at[i], p_r.at[i], device(c_=1 - c))
    for i in range(RING):
        arrived(prem.at[i], p_s.at[i], p_r.at[i])

    def own_terms(i, carry):
        t = terms(i, c)
        for n in range(RING):
            part[i, n] = (t[:, n * LANES : (n + 1) * LANES] + prem[i, n].astype(F32)).astype(BF)
        return carry

    lax.fori_loop(0, RING, own_terms, 0)

    def view(h, t, start, size):
        r = pl.ds(h * two + start, size)
        return (slice(None), t, r, slice(None)) if h == 0 else (t, slice(None), r, slice(None))

    first = [x, y]
    second = [y, x]

    def hop(h, stage, step):
        return device(x_=at(x, step)) if (h == 0) == (stage == 0) else device(y_=at(y, step))

    for h in (0, 1):
        far = at(first[h], FAR)
        put(part.at[view(h, far, 0, four)], relay.at[h, 0], q_s.at[h, 0], q_r.at[h, 0], hop(h, 0, RIGHT))
        put(part.at[view(h, far, four, four)], relay.at[h, 1], q_s.at[h, 1], q_r.at[h, 1], hop(h, 0, LEFT))
    for h in (0, 1):
        put(
            part.at[view(h, at(first[h], RIGHT), four, four)], joined.at[h, 0, :, pl.ds(four, four)],
            j_s.at[h, 0, 0], j_r.at[h, 0, 0], hop(h, 0, RIGHT),
        )
        put(
            part.at[view(h, at(first[h], LEFT), 0, four)], joined.at[h, 1, :, pl.ds(0, four)],
            j_s.at[h, 1, 0], j_r.at[h, 1, 0], hop(h, 0, LEFT),
        )

    def gradients(i, squares):
        pair = [2 * i, 2 * i + 1]
        cols = pl.ds(pl.multiple_of(i * 2 * LANES, 2 * LANES), 2 * LANES)
        xs = jnp.concatenate([slots[0, s] for s in pair], axis=1)
        gs = jnp.concatenate([slots[1, s] for s in pair], axis=1)
        g = dot(delta[...], xs, ((1,), (0,)))
        grads[pl.ds(0, 2 * units), cols] = g.astype(BF)
        squares += jnp.sum((g * g).reshape(2 * units // 8, 8, 2 * LANES), axis=0)
        g = dot(hid_t[pl.ds(0, units), :], gs, ((1,), (0,)))
        grads[pl.ds(2 * units, units), cols] = g.astype(BF)
        return squares + jnp.sum((g * g).reshape(units // 8, 8, 2 * LANES), axis=0)

    pairs = slots.shape[1] // 2
    squares = lax.fori_loop(0, pairs // 2, gradients, jnp.zeros((8, 2 * LANES), F32))

    for h in (0, 1):
        arrived(relay.at[h, 0], q_s.at[h, 0], q_r.at[h, 0])
        v = view(h, at(first[h], RIGHT), 0, four)
        part[v] = (part[v].astype(F32) + relay[h, 0].astype(F32)).astype(BF)
        arrived(relay.at[h, 1], q_s.at[h, 1], q_r.at[h, 1])
        u = view(h, at(first[h], LEFT), four, four)
        part[u] = (part[u].astype(F32) + relay[h, 1].astype(F32)).astype(BF)
        put(part.at[v], joined.at[h, 0, :, pl.ds(0, four)], j_s.at[h, 0, 1], j_r.at[h, 0, 1], hop(h, 0, RIGHT))
        put(part.at[u], joined.at[h, 1, :, pl.ds(four, four)], j_s.at[h, 1, 1], j_r.at[h, 1, 1], hop(h, 0, LEFT))

    squares = lax.fori_loop(pairs // 2, pairs, gradients, squares)
    stores = [
        pltpu.make_async_copy(grads.at[pl.ds(n * units, units)], out, local.at[5 + n])
        for n, out in enumerate((gate_out, up_out, down_out))
    ]
    for store in stores:
        store.start()

    def share(stage, value, devices, base):
        sq_send[stage] = value
        for n, dev in enumerate(devices):
            put(sq_send.at[stage], sq_recv.at[base + n], sq_s.at[base + n], sq_r.at[base + n], dev)

    def gathered(value, base, n):
        for i in range(base, base + n):
            arrived(sq_recv.at[i], sq_s.at[i], sq_r.at[i])
            value = value + sq_recv[i]
        return value

    value = squares[:, :LANES] + squares[:, LANES:]
    share(0, value, [device(c_=1 - c)], 0)

    for h in (0, 1):
        for n, starts in enumerate(((four, 0), (0, four))):
            for piece, start in enumerate(starts):
                arrived(joined.at[h, n, :, pl.ds(start, four)], j_s.at[h, n, piece], j_r.at[h, n, piece])
        v = view(h, first[h], 0, two)
        half[h] = (part[v].astype(F32) + joined[h, 0].astype(F32) + joined[h, 1].astype(F32)).astype(BF)
        for j in (1, 2, 3):
            put(half.at[h, at(second[h], j)], last.at[h, j - 1], l_s.at[h, j - 1], l_r.at[h, j - 1], hop(h, 1, j))
    value = gathered(value, 0, 1)
    share(1, value, [device(x_=at(x, s)) for s in (1, 2, 3)], 1)

    for h in (0, 1):
        summed = half[h, second[h]].astype(F32)
        for j in (1, 2, 3):
            arrived(last.at[h, j - 1], l_s.at[h, j - 1], l_r.at[h, j - 1])
            summed = summed + last[h, j - 1].astype(F32)
        final[pl.ds(h * two, two), :] = summed.astype(BF)
    for j in range(1, experts):
        to = (z + j) % experts
        to_rows = pl.ds(pl.multiple_of(to * cap, cap), cap)
        put(final.at[to_rows], back.at[own_rows], k_s.at[j - 1], k_r.at[j - 1], device(z_=to))
    value = gathered(value, 1, 3)
    share(2, value, [device(y_=at(y, s)) for s in (1, 2, 3)], 4)
    back[own_rows, :] = final[own_rows, :]
    value = gathered(value, 4, 3)
    share(3, value, [device(z_=(z + j) % experts) for j in range(1, experts)], 7)
    for j in range(1, experts):
        source = (z + experts - j) % experts
        from_rows = pl.ds(pl.multiple_of(source * cap, cap), cap)
        arrived(back.at[from_rows], k_s.at[j - 1], k_r.at[j - 1])
    picked = [dot(hot_t[k], back[...], ((1,), (0,))) for k in (0, 1)]
    layer_out[...] = (weight[:, 0:1] * picked[0] + weight[:, 1:2] * picked[1]).astype(BF)
    value = gathered(value, 7, experts - 1)
    inv_out[...] = jnp.broadcast_to(
        lax.rsqrt(jnp.sum(value, keepdims=True) / total + 1e-06), inv_out.shape
    )
    for store in stores:
        store.wait()
    for copy in started:
        copy.wait_send()


def solution(mesh):
    experts = mesh.shape["expert"]
    groups = mesh.shape["dp"] * mesh.shape["ffn"]

    def on_device(tokens, expert_ids, route_weight, cotangent, w_gate, w_up, w_down):
        rows, features = tokens.shape
        units = w_gate.shape[1]
        padded = -(-units // LANES) * LANES
        count = experts * rows // 2
        two, four = count // 2, count // 4
        total = 3.0 * experts * units * groups * features
        vmem, anywhere = pl.BlockSpec(memory_space=pltpu.VMEM), pl.BlockSpec(memory_space=pl.ANY)
        dma = pltpu.SemaphoreType.DMA
        gate, up, down, inv, layer = pl.pallas_call(
            functools.partial(body, experts=experts, total=total),
            out_shape=[jax.ShapeDtypeStruct((units, features), BF)] * 3
            + [jax.ShapeDtypeStruct((8, LANES), F32), jax.ShapeDtypeStruct((rows, LANES), BF)],
            in_specs=[vmem, vmem] + [anywhere] * 5,
            out_specs=[anywhere] * 3 + [vmem, vmem],
            scratch_shapes=[
                pltpu.VMEM((rows, LANES), BF),
                pltpu.VMEM((rows, LANES), BF),
                pltpu.VMEM((2, count, rows), BF),
                pltpu.VMEM((2, rows, count), BF),
                pltpu.VMEM((2, count, LANES), BF),
                pltpu.VMEM((2, groups, count, LANES), BF),
                pltpu.VMEM((2 * units, features), BF),
                pltpu.VMEM((padded, features), BF),
                pltpu.VMEM((3 * units, count), F32),
                pltpu.VMEM((padded, count), BF),
                pltpu.VMEM((count, padded), BF),
                pltpu.VMEM((2 * units, count), BF),
                pltpu.VMEM((3 * units, features), BF),
                pltpu.VMEM((RING, RING, count, LANES), BF),
                pltpu.VMEM((RING, RING, count, LANES), BF),
                pltpu.VMEM((RING, RING, count, LANES), BF),
                pltpu.VMEM((2, 2, RING, four, LANES), BF),
                pltpu.VMEM((2, 2, RING, two, LANES), BF),
                pltpu.VMEM((2, RING, two, LANES), BF),
                pltpu.VMEM((2, 3, two, LANES), BF),
                pltpu.VMEM((count, LANES), BF),
                pltpu.VMEM((count, LANES), BF),
                pltpu.VMEM((4, 8, LANES), F32),
                pltpu.VMEM((6 + experts, 8, LANES), F32),
                dma((8,)),
                dma((2, experts - 1)), dma((2, experts - 1)),
                dma((2, 4)), dma((2, 4)),
                dma((2, RING, 4)), dma((2, RING, 4)),
                dma((2, RING, RING)), dma((2, RING, RING)),
                dma((RING,)), dma((RING,)),
                dma((2, 2)), dma((2, 2)),
                dma((2, 2, 2)), dma((2, 2, 2)),
                dma((2, 3)), dma((2, 3)),
                dma((experts - 1,)), dma((experts - 1,)),
                dma((6 + experts,)), dma((6 + experts,)),
            ],
            compiler_params=pltpu.CompilerParams(
                collective_id=0, has_side_effects=True, vmem_limit_bytes=60 * 1024 * 1024
            ),
            name="layer",
        )(expert_ids.T, route_weight, tokens, cotangent, w_gate, w_up, w_down)
        scale = inv[0, 0]
        return (
            layer,
            (gate.astype(F32) * scale).astype(BF)[None],
            (up.astype(F32) * scale).astype(BF)[None],
            (down.astype(F32) * scale).astype(BF)[None],
        )

    token, hidden = P("expert", None), P("expert", ("dp", "ffn"), None)
    return jax.shard_map(
        on_device,
        mesh=mesh,
        in_specs=(token, token, token, token, hidden, hidden, hidden),
        out_specs=(P("expert", ("dp", "ffn")), hidden, hidden, hidden),
        check_vma=False,
    )
```

time: 265 us -> 90.2 us (0.34)
  blocking collectives: 115 us -> 0 us
  Pallas kernels: 0 us -> 78.4 us
  waiting for transfers between devices: 65.6 us -> 0 us
  matrix products: 31.3 us -> 0 us
  between operations: 16.8 us -> 0.64 us
  starting transfers between devices: 11.2 us -> 0 us
  other arithmetic: 18.2 us -> 7.6 us
    psum x1 -> x0, blocking collectives: 95.2 us -> none  [on_device(): lax.psum(squares_of(grad_gate) + squares_of(grad_up) + squares_of(grad_do...]
    pallas_call x0 -> x1, Pallas kernels: none -> 78.4 us  [on_device(): pl.pallas_call(functools.partial(body, experts=experts, total=total), out...]
    all_gather x1 -> x0, waiting for transfers between devices: 60 us -> none  [side_by_side(): lax.all_gather(both, axis, axis=dim, tiled=True)]
    dot_general x10 -> x0, matrix products: 31.3 us -> none  [the longest x5 18.1 us: against_rows(): lax.dot_general(left_rows, right_rows, (((0,), (0,)), ((), ())), preferre...]
    all_to_all x1 -> x0, blocking collectives: 20.1 us -> none  [sent_together(): lax.all_to_all(both, axis, split_axis=split_dim, concat_axis=concat_dim,...]
    all_to_all x2 -> x0, starting transfers between devices: 11.1 us -> none  [the longest x1 6.28 us: sum_at_owner(): tiles = lax.all_to_all(split_up(x, dim, devices), axis, 0, 0, tiled=True)]
    all_to_all x2 -> x0, waiting for transfers between devices: 5.57 us -> none  [the longest x1 5.57 us: on_device(): lax.all_to_all(summed, 'expert', split_axis=0, concat_axis=0, tiled=True)]
    reduce_sum x3 -> x0, other arithmetic: 5.04 us -> none  [the longest x1 3.46 us: sum_at_owner(): return jnp.sum(tiles.astype(jnp.float32), axis=0)]
  transfers between devices with their start and end apart: 3 -> 0, of which waited for: 2 -> 0; matrix products, arithmetic and copies ran while one was open for 11% -> 0% of each run, Pallas kernels for 0% -> 0%
where the time goes in v2:
time: 90.2 us; the launch traced here: 89.9 us
  Pallas kernels  78.4 us (87%)
  other arithmetic  7.6 us (8%)
  local copies, waits for them, and re-layouts  3.23 us (4%)
    pallas_call x1, Pallas kernels, on_device(): pl.pallas_call(functools.partial(body, experts=experts, total=total), out...  78.4 us
    broadcast_in_dim x1, other arithmetic, on_device(): (down.astype(F32) * scale).astype(BF)[None]  4.2 us
    broadcast_in_dim x1, other arithmetic, on_device(): (gate.astype(F32) * scale).astype(BF)[None]  3.4 us
    unnamed x8, local copies, waits for them, and re-layouts  2.04 us

profile of v2, /device:TPU:2, one launch (start us, length us, event | category | flops | bytes accessed | tf_op | source)
XLA Modules:
  0.0 89.9 jit_solution(17740069642115532842)
XLA Ops:
  0.6 1.4 %copy.11.weight = f32[128,2]{1,0:T(8,128)} copy(f32[128,2]{0,1:T(2,128)} %param.9) | data formatting | bytes 2048 | tf_op args[2]
  2.0 78.4 %layer.1 = (bf16[224,4096]{1,0:T(8,128)(2,1)}, bf16[224,4096]{1,0:T(8,128)(2,1)}, bf16[224,4096]{1,0:T(8,128)(2,1)}, f32[8,128]{1,0:T(8,128)}, bf16[128,128]{1,0:T(8,128)(2,1)}) custom-call(s32[2,128]{1,0:T(2,128)} %bitcast.8, f32[128,2]{1,0:T(8,128)} %copy.11.weight, bf16[128,4096]{1,0:T(8,128)(2,1)} %tokens.1, bf16[128,4096]{1,0:T(8,128)(2,1)} %cotangent.1, ...), custom_call_target="tpu_custom_call" | custom-call | tf_op jit(solution)/shard_map/layer/pallas_call | solution.py:399
  80.5 1.2 %slice.3 = f32[1,1]{1,0:T(1,128)} slice(f32[8,128]{1,0:T(8,128)} %get-tuple-element.11), slice={[0:1], [0:1]} | slice | bytes 8 | tf_op jit(solution)/shard_map/slice | solution.py:447
  81.7 0.0 copy-start
  81.7 0.0 copy-start.1
  81.7 4.2 %fusion.2 = bf16[1,224,4096]{2,1,0:T(8,128)(2,1)} fusion(bf16[224,4096]{1,0:T(8,128)(2,1)} %get-tuple-element.13, f32[]{:T(128)} %bitcast.1), kind=kLoop, calls=%fused_computation.5 | loop fusion | flops 2752512 | bytes 3670020 | tf_op jit(solution)/shard_map/broadcast_in_dim | solution.py:452
  85.9 0.0 copy-done
  85.9 0.0 copy-done.1
  85.9 0.0 copy-start.2
  85.9 3.4 %fusion = (bf16[1,224,4096]{2,1,0:T(8,128)(2,1)}, bf16[1,224,4096]{2,1,0:T(8,128)(2,1)}) fusion(bf16[224,4096]{1,0:T(8,128)(2,1)S(1)} %copy-done, f32[]{:T(128)} %bitcast.1, bf16[224,4096]{1,0:T(8,128)(2,1)S(1)} %copy-done.1), kind=kLoop, calls=%fused_computation.3 | loop fusion | flops 5505024 | bytes 7340036 | tf_op jit(solution)/shard_map/broadcast_in_dim | solution.py:450
  89.3 0.0 copy-done.2
  89.3 0.6 copy.13
Async XLA Ops:
  81.7 4.2 %copy-start = (bf16[224,4096]{1,0:T(8,128)(2,1)S(1)}, bf16[224,4096]{1,0:T(8,128)(2,1)}, u32[]{:S(2)}) copy-start(bf16[224,4096]{1,0:T(8,128)(2,1)} %get-tuple-element.10) | copy-start | bytes 5505028
  81.7 4.2 %copy-start.1 = (bf16[224,4096]{1,0:T(8,128)(2,1)S(1)}, bf16[224,4096]{1,0:T(8,128)(2,1)}, u32[]{:S(2)}) copy-start(bf16[224,4096]{1,0:T(8,128)(2,1)} %get-tuple-element.12) | copy-start | bytes 5505028
  85.9 3.4 %copy-start.2 = (bf16[128,128]{1,0:T(8,128)(2,1)S(1)}, bf16[128,128]{1,0:T(8,128)(2,1)}, u32[]{:S(2)}) copy-start(bf16[128,128]{1,0:T(8,128)(2,1)} %get-tuple-element.20) | copy-start | bytes 98308

commit v3 on v2

--- a/solution.py
+++ b/solution.py
@@ -11,6 +11,9 @@
 BF = jnp.bfloat16
 F32 = jnp.float32
 LANES = 128
+BLOCK = 32
+VMEM = 36 * 1024 * 1024
+SCALE_VMEM = 20 * 1024 * 1024
 RING = 4
 LEFT, RIGHT, FAR = 3, 1, 2
 EVENTS = (
@@ -31,8 +34,8 @@
 
 def body(
     ids, weight, tokens, cotangent, w_gate, w_up, w_down,
-    gate_out, up_out, down_out, inv_out, layer_out,
-    tok, cot, hot, hot_t, send, slots, w_gu, w_d, acc, hid_t, hid, delta, grads,
+    grads, inv_out, layer_out,
+    tok, cot, hot, hot_t, send, slots, w_gu, w_d, acc, hid_t, hid, delta, weights,
     psend, prem, part, relay, joined, half, last, final, back, sq_send, sq_recv,
     local, z_s, z_r, a_s, a_r, b_s, b_r, d_s, d_r, p_s, p_r, q_s, q_r, j_s, j_r,
     l_s, l_r, k_s, k_r, sq_s, sq_r,
@@ -106,16 +109,18 @@
     loads[1].wait()
     send[0] = dot(hot[0] + hot[1], tok[...], ((1,), (0,))).astype(BF)
     wide = cot[...].astype(F32)
-    scaled = [(weight[:, k : k + 1] * wide).astype(BF) for k in (0, 1)]
+    for k in (0, 1):
+        weights[k] = jnp.broadcast_to(weight[k : k + 1, :], (LANES, rows)).T
+    scaled = [(weights[k] * wide).astype(BF) for k in (0, 1)]
     send[1] = (
         dot(hot[0], scaled[0], ((1,), (0,))) + dot(hot[1], scaled[1], ((1,), (0,)))
     ).astype(BF)
     own_rows = pl.ds(pl.multiple_of(z * cap, cap), cap)
     pl.semaphore_wait(barrier, len(peers))
-    for j in range(1, experts):
-        to = (z + j) % experts
-        to_rows = pl.ds(pl.multiple_of(to * cap, cap), cap)
-        for p in (0, 1):
+    for p in (0, 1):
+        for j in sorted(range(1, experts), key=lambda j: -min(j, experts - j)):
+            to = (z + j) % experts
+            to_rows = pl.ds(pl.multiple_of(to * cap, cap), cap)
             put(
                 send.at[p, to_rows], slots.at[p, mine, own_rows],
                 z_s.at[p, j - 1], z_r.at[p, j - 1], device(z_=to),
@@ -131,10 +136,11 @@
         hot_t[k] = hot[k].astype(F32).T.astype(BF)
     for load in loads[2:]:
         load.wait()
-    for j in range(1, experts):
-        source = (z + experts - j) % experts
-        from_rows = pl.ds(pl.multiple_of(source * cap, cap), cap)
-        for p in (0, 1):
+
+    def await_tokens(p):
+        for j in range(1, experts):
+            source = (z + experts - j) % experts
+            from_rows = pl.ds(pl.multiple_of(source * cap, cap), cap)
             arrived(slots.at[p, mine, from_rows], z_s.at[p, j - 1], z_r.at[p, j - 1])
 
     def place(p, k, m):
@@ -201,31 +207,40 @@
             for p in (0, 1):
                 accumulate(p, k, m)
 
-    previous = None
-    for event in EVENTS:
+    def take(p, k, m):
+        await_slice(p, k, m)
+        s = own_slice(p, k, m)
+        if m == 0:
+            if k == 0:
+                both_ways(p, 0, s, *sem_a(p))
+            elif k != FAR:
+                onward(p, 0, s, k, *sem_a(p))
+        elif m != FAR:
+            onward(p, 1, s, m, *sem_b(p, k))
+
+    def pass_on(p, k, m):
+        s = own_slice(p, k, m)
+        if m == 0:
+            both_ways(p, 1, s, *sem_b(p, k))
+        put(whole(p, s), whole(p, s), d_s.at[p, k, m], d_r.at[p, k, m], device(c_=1 - c))
+
+    for p in (0, 1):
+        await_tokens(p)
+        take(p, 0, 0)
+        pass_on(p, 0, 0)
+    previous = EVENTS[0]
+    for event in EVENTS[1:]:
         for k, m in event:
             for p in (0, 1):
-                await_slice(p, k, m)
-                s = own_slice(p, k, m)
-                if m == 0:
-                    if k == 0:
-                        both_ways(p, 0, s, *sem_a(p))
-                    elif k != FAR:
-                        onward(p, 0, s, k, *sem_a(p))
-                elif m != FAR:
-                    onward(p, 1, s, m, *sem_b(p, k))
+                take(p, k, m)
         for k, m in event:
             for p in (0, 1):
-                s = own_slice(p, k, m)
-                if m == 0:
-                    both_ways(p, 1, s, *sem_b(p, k))
-                put(whole(p, s), whole(p, s), d_s.at[p, k, m], d_r.at[p, k, m], device(c_=1 - c))
-        if previous is not None:
-            finish(previous)
+                pass_on(p, k, m)
+        finish(previous)
         previous = event
     finish(previous)
 
-    block = 32
+    block = BLOCK
 
     def activate(i, carry):
         r = pl.multiple_of(i * block, block)
@@ -250,25 +265,16 @@
         cols = pl.ds(pl.multiple_of((2 * y_ + c_) * width, width), width)
         return dot(hid[...], w_d[:, cols], ((1,), (0,)))
 
-    def partner_terms(i, carry):
+    for i in range(RING):
         t = terms(i, 1 - c)
         for n in range(RING):
             psend[i, n] = t[:, n * LANES : (n + 1) * LANES].astype(BF)
-        return carry
-
-    lax.fori_loop(0, RING, partner_terms, 0)
-    for i in range(RING):
         put(psend.at[i], prem.at[i], p_s.at[i], p_r.at[i], device(c_=1 - c))
     for i in range(RING):
+        t = terms(i, c)
         arrived(prem.at[i], p_s.at[i], p_r.at[i])
-
-    def own_terms(i, carry):
-        t = terms(i, c)
         for n in range(RING):
             part[i, n] = (t[:, n * LANES : (n + 1) * LANES] + prem[i, n].astype(F32)).astype(BF)
-        return carry
-
-    lax.fori_loop(0, RING, own_terms, 0)
 
     def view(h, t, start, size):
         r = pl.ds(h * two + start, size)
@@ -300,10 +306,10 @@
         xs = jnp.concatenate([slots[0, s] for s in pair], axis=1)
         gs = jnp.concatenate([slots[1, s] for s in pair], axis=1)
         g = dot(delta[...], xs, ((1,), (0,)))
-        grads[pl.ds(0, 2 * units), cols] = g.astype(BF)
+        grads[pl.ds(0, 2 * units), cols] = g
         squares += jnp.sum((g * g).reshape(2 * units // 8, 8, 2 * LANES), axis=0)
         g = dot(hid_t[pl.ds(0, units), :], gs, ((1,), (0,)))
-        grads[pl.ds(2 * units, units), cols] = g.astype(BF)
+        grads[pl.ds(2 * units, units), cols] = g
         return squares + jnp.sum((g * g).reshape(units // 8, 8, 2 * LANES), axis=0)
 
     pairs = slots.shape[1] // 2
@@ -320,12 +326,6 @@
         put(part.at[u], joined.at[h, 1, :, pl.ds(four, four)], j_s.at[h, 1, 1], j_r.at[h, 1, 1], hop(h, 0, LEFT))
 
     squares = lax.fori_loop(pairs // 2, pairs, gradients, squares)
-    stores = [
-        pltpu.make_async_copy(grads.at[pl.ds(n * units, units)], out, local.at[5 + n])
-        for n, out in enumerate((gate_out, up_out, down_out))
-    ]
-    for store in stores:
-        store.start()
 
     def share(stage, value, devices, base):
         sq_send[stage] = value
@@ -372,15 +372,34 @@
         from_rows = pl.ds(pl.multiple_of(source * cap, cap), cap)
         arrived(back.at[from_rows], k_s.at[j - 1], k_r.at[j - 1])
     picked = [dot(hot_t[k], back[...], ((1,), (0,))) for k in (0, 1)]
-    layer_out[...] = (weight[:, 0:1] * picked[0] + weight[:, 1:2] * picked[1]).astype(BF)
+    layer_out[...] = (weights[0] * picked[0] + weights[1] * picked[1]).astype(BF)
     value = gathered(value, 7, experts - 1)
     inv_out[...] = jnp.broadcast_to(
         lax.rsqrt(jnp.sum(value, keepdims=True) / total + 1e-06), inv_out.shape
     )
-    for store in stores:
-        store.wait()
     for copy in started:
         copy.wait_send()
+
+
+def scale_body(grads, inv, layer, gate_out, up_out, down_out, layer_out, scaled, sems):
+    units = gate_out.shape[0]
+    blocks = units // BLOCK
+    scale = inv[0:1, 0:1]
+    for n, out in enumerate((gate_out, up_out, down_out)):
+
+        def step(i, carry):
+            r = pl.multiple_of(i * BLOCK, BLOCK)
+            rows = pl.ds(n * units + r, BLOCK)
+            scaled[rows, :] = (grads[rows, :] * scale).astype(BF)
+            pltpu.make_async_copy(scaled.at[rows], out.at[pl.ds(r, BLOCK)], sems.at[n * blocks + i]).start()
+            return carry
+
+        lax.fori_loop(0, blocks, step, 0)
+    layer_out[...] = layer[...]
+    for n, out in enumerate((gate_out, up_out, down_out)):
+        for i in range(blocks):
+            rows = pl.ds(n * units + i * BLOCK, BLOCK)
+            pltpu.make_async_copy(scaled.at[rows], out.at[pl.ds(i * BLOCK, BLOCK)], sems.at[n * blocks + i]).wait()
 
 
 def solution(mesh):
@@ -394,14 +413,17 @@
         count = experts * rows // 2
         two, four = count // 2, count // 4
         total = 3.0 * experts * units * groups * features
-        vmem, anywhere = pl.BlockSpec(memory_space=pltpu.VMEM), pl.BlockSpec(memory_space=pl.ANY)
+        vmem, anywhere = pl.BlockSpec(memory_space=pltpu.VMEM), pl.BlockSpec(memory_space=pltpu.HBM)
         dma = pltpu.SemaphoreType.DMA
-        gate, up, down, inv, layer = pl.pallas_call(
+        grads, inv, layer = pl.pallas_call(
             functools.partial(body, experts=experts, total=total),
-            out_shape=[jax.ShapeDtypeStruct((units, features), BF)] * 3
-            + [jax.ShapeDtypeStruct((8, LANES), F32), jax.ShapeDtypeStruct((rows, LANES), BF)],
+            out_shape=[
+                jax.ShapeDtypeStruct((3 * units, features), F32),
+                jax.ShapeDtypeStruct((8, LANES), F32),
+                jax.ShapeDtypeStruct((rows, LANES), BF),
+            ],
             in_specs=[vmem, vmem] + [anywhere] * 5,
-            out_specs=[anywhere] * 3 + [vmem, vmem],
+            out_specs=[vmem] * 3,
             scratch_shapes=[
                 pltpu.VMEM((rows, LANES), BF),
                 pltpu.VMEM((rows, LANES), BF),
@@ -415,7 +437,7 @@
                 pltpu.VMEM((padded, count), BF),
                 pltpu.VMEM((count, padded), BF),
                 pltpu.VMEM((2 * units, count), BF),
-                pltpu.VMEM((3 * units, features), BF),
+                pltpu.VMEM((2, rows, LANES), F32),
                 pltpu.VMEM((RING, RING, count, LANES), BF),
                 pltpu.VMEM((RING, RING, count, LANES), BF),
                 pltpu.VMEM((RING, RING, count, LANES), BF),
@@ -427,7 +449,7 @@
                 pltpu.VMEM((count, LANES), BF),
                 pltpu.VMEM((4, 8, LANES), F32),
                 pltpu.VMEM((6 + experts, 8, LANES), F32),
-                dma((8,)),
+                dma((5,)),
                 dma((2, experts - 1)), dma((2, experts - 1)),
                 dma((2, 4)), dma((2, 4)),
                 dma((2, RING, 4)), dma((2, RING, 4)),
@@ -440,17 +462,21 @@
                 dma((6 + experts,)), dma((6 + experts,)),
             ],
             compiler_params=pltpu.CompilerParams(
-                collective_id=0, has_side_effects=True, vmem_limit_bytes=60 * 1024 * 1024
+                collective_id=0, has_side_effects=True, vmem_limit_bytes=VMEM
             ),
             name="layer",
-        )(expert_ids.T, route_weight, tokens, cotangent, w_gate, w_up, w_down)
-        scale = inv[0, 0]
-        return (
-            layer,
-            (gate.astype(F32) * scale).astype(BF)[None],
-            (up.astype(F32) * scale).astype(BF)[None],
-            (down.astype(F32) * scale).astype(BF)[None],
-        )
+        )(expert_ids.T, route_weight.T, *[pltpu.with_memory_space_constraint(a, pltpu.HBM) for a in (tokens, cotangent, w_gate, w_up, w_down)])
+        gate, up, down, layer = pl.pallas_call(
+            scale_body,
+            out_shape=[jax.ShapeDtypeStruct((units, features), BF)] * 3
+            + [jax.ShapeDtypeStruct((rows, LANES), BF)],
+            in_specs=[vmem] * 3,
+            out_specs=[anywhere] * 3 + [vmem],
+            scratch_shapes=[pltpu.VMEM((3 * units, features), BF), dma((3 * (units // BLOCK),))],
+            compiler_params=pltpu.CompilerParams(vmem_limit_bytes=SCALE_VMEM),
+            name="scale",
+        )(grads, inv, layer)
+        return layer, gate[None], up[None], down[None]
 
     token, hidden = P("expert", None), P("expert", ("dp", "ffn"), None)
     return jax.shard_map(

time: 90.2 us -> 79.1 us (0.88)
  other arithmetic: 7.6 us -> 0 us
  local copies, waits for them, and re-layouts: 3.23 us -> 1.35 us
  Pallas kernels: 78.4 us -> 77 us
    broadcast_in_dim x2 -> x0, other arithmetic: 7.6 us -> none  [the longest x1 4.2 us: on_device(): (down.astype(F32) * scale).astype(BF)[None]]
    pallas_call x1, Pallas kernels: 78.4 us -> 73.7 us  [on_device(): pl.pallas_call(functools.partial(body, experts=experts, total=total), out...]
    pallas_call x0 -> x1, Pallas kernels: none -> 3.28 us  [on_device(): pl.pallas_call(scale_body, out_shape=[jax.ShapeDtypeStruct((units, featur...]
    slice x1 -> x0, local copies, waits for them, and re-layouts: 1.19 us -> none  [on_device(): scale = inv[0, 0]]
    unnamed x8 -> x4, local copies, waits for them, and re-layouts: 2.04 us -> 1.35 us
where the time goes in v3:
time: 79.1 us; the launch traced here: 79 us
  Pallas kernels  77 us (97%)
  local copies, waits for them, and re-layouts  1.35 us (2%)
    pallas_call x1, Pallas kernels, on_device(): pl.pallas_call(functools.partial(body, experts=experts, total=total), out...  73.7 us
    pallas_call x1, Pallas kernels, on_device(): pl.pallas_call(scale_body, out_shape=[jax.ShapeDtypeStruct((units, featur...  3.28 us

profile of v3, /device:TPU:2, one launch (start us, length us, event | category | flops | bytes accessed | tf_op | source)
XLA Modules:
  0.0 79.0 jit_solution(11524616043288107780)
XLA Ops:
  0.6 0.0 copy-start
  0.6 0.7 copy-done
  1.3 0.0 copy-start.1
  1.3 0.7 copy-done.1
  2.0 73.7 %layer.1 = (f32[672,4096]{1,0:T(8,128)S(1)}, f32[8,128]{1,0:T(8,128)S(1)}, bf16[128,128]{1,0:T(8,128)(2,1)S(1)}) custom-call(s32[2,128]{1,0:T(2,128)S(1)} %bitcast.5, f32[2,128]{1,0:T(2,128)S(1)} %bitcast.6, bf16[128,4096]{1,0:T(8,128)(2,1)} %tokens.1, bf16[128,4096]{1,0:T(8,128)(2,1)} %cotangent.1, bf16[1,224,4096]{2,1,0:T(8,128)(2,1)} %w_gate.1, ...), custom_call_target="tpu_custom_call" | custom-call | tf_op jit(solution)/shard_map/layer/pallas_call | solution.py:418
  75.7 3.3 %scale.1 = (bf16[224,4096]{1,0:T(8,128)(2,1)}, bf16[224,4096]{1,0:T(8,128)(2,1)}, bf16[224,4096]{1,0:T(8,128)(2,1)}, bf16[128,128]{1,0:T(8,128)(2,1)}) custom-call(f32[672,4096]{1,0:T(8,128)S(1)} %get-tuple-element.11.grads, f32[8,128]{1,0:T(8,128)S(1)} %get-tuple-element.12.inv, bf16[128,128]{1,0:T(8,128)(2,1)S(1)} %get-tuple-element.13.layer), custom_call_target="tpu_custom_call" | custom-call | tf_op jit(solution)/shard_map/scale/pallas_call | solution.py:469
Async XLA Ops:
  0.6 0.7 copy-start
  1.3 0.7 copy-start.1

commit v4 on v3

v4 whole, which is shorter than its diff:
```python
import functools

import jax
import jax.numpy as jnp
from jax import lax
from jax.experimental import pallas as pl
from jax.experimental.pallas import tpu as pltpu
from jax.sharding import PartitionSpec as P

MESH = pl.DeviceIdType.MESH
BF = jnp.bfloat16
F32 = jnp.float32
LANES = 128
BLOCK = 32
VMEM = 46 * 1024 * 1024
COPY_VMEM = 4 * 1024 * 1024
RING = 4
LEFT, RIGHT, FAR = 3, 1, 2
EVENTS = (
    ((0, 0),),
    ((LEFT, 0), (RIGHT, 0)),
    ((0, LEFT), (0, RIGHT)),
    ((FAR, 0),),
    ((LEFT, LEFT), (LEFT, RIGHT), (RIGHT, LEFT), (RIGHT, RIGHT)),
    ((0, FAR),),
    ((FAR, LEFT), (FAR, RIGHT)),
    ((FAR, FAR), (LEFT, FAR), (RIGHT, FAR)),
)
DIRECT = ((0, 0), (FAR, 0), (FAR, FAR))


def dot(a, b, dims):
    return lax.dot_general(a, b, (dims, ((), ())), preferred_element_type=F32)


def body(
    ids_in, weight_in, tokens, cotangent, w_gate, w_up, w_down,
    scaled_out, layer_out,
    ids, weight, grads, tok, cot, hot, hot_t, send, slots, w_gu, w_d, acc, hid_t, hid, delta, weights,
    psend, prem, part, relay, joined, half, last, final, back, sq_send, sq_recv,
    local, z_s, z_r, a_s, a_r, b_s, b_r, d_s, d_r, p_s, p_r, q_s, q_r, j_s, j_r,
    l_s, l_r, k_s, k_r, sq_s, sq_r,
    *, experts, total,
):
    dp, z, x = lax.axis_index("dp"), lax.axis_index("expert"), lax.axis_index("ffn")
    y, c = dp // 2, dp % 2
    cap = tok.shape[1] // 2
    count = experts * cap
    units = w_gate.shape[1]
    two, four = count // 2, count // 4

    def at(v, step):
        return (v + step) % RING

    def device(x_=x, y_=y, c_=c, z_=z):
        return {"dp": y_ * 2 + c_, "expert": z_, "ffn": x_}

    def slice_of(x_, y_, c_):
        return (2 * y_ + c_) * RING + x_

    started = []

    def put(src, dst, s_sem, r_sem, dev):
        copy = pltpu.make_async_remote_copy(
            src_ref=src, dst_ref=dst, send_sem=s_sem, recv_sem=r_sem, device_id=dev, device_id_type=MESH
        )
        copy.start()
        started.append(copy)

    def arrived(dst, s_sem, r_sem):
        pltpu.make_async_remote_copy(
            src_ref=dst, dst_ref=dst, send_sem=s_sem, recv_sem=r_sem,
            device_id=device(c_=1 - c), device_id_type=MESH,
        ).wait_recv()

    def place(p, k, m):
        return (at(x, k), at(y, m)) if p == 0 else (at(x, m), at(y, k))

    def own_slice(p, k, m):
        return slice_of(*place(p, k, m), c)

    def columns(p, e):
        return pl.ds(pl.multiple_of(own_slice(p, *DIRECT[e]) * LANES, LANES), LANES)

    loads = [
        pltpu.make_async_copy(ids_in, ids, local.at[0]),
        pltpu.make_async_copy(weight_in, weight, local.at[1]),
    ]
    for e in range(len(DIRECT)):
        loads.append(pltpu.make_async_copy(tokens.at[:, columns(0, e)], tok.at[e], local.at[2 + 2 * e]))
        loads.append(pltpu.make_async_copy(cotangent.at[:, columns(1, e)], cot.at[e], local.at[3 + 2 * e]))
    loads += [
        pltpu.make_async_copy(w_gate.at[0], w_gu.at[pl.ds(0, units)], local.at[8]),
        pltpu.make_async_copy(w_up.at[0], w_gu.at[pl.ds(units, units)], local.at[9]),
        pltpu.make_async_copy(w_down.at[0], w_d.at[pl.ds(0, units)], local.at[10]),
    ]
    for load in loads[:8]:
        load.start()

    peers = [device(c_=1 - c)]
    peers += [device(x_=at(x, s)) for s in (1, 2, 3)] + [device(y_=at(y, s)) for s in (1, 2, 3)]
    peers += [device(z_=(z + j) % experts) for j in range(1, experts)]
    barrier = pltpu.get_barrier_semaphore()
    for peer in peers:
        pl.semaphore_signal(barrier, inc=1, device_id=peer, device_id_type=MESH)

    for load in loads[:2]:
        load.wait()
    rows = tok.shape[1]
    names = lax.broadcasted_iota(jnp.int32, (experts, rows), 0)
    chosen = [names == ids[k : k + 1, :] for k in (0, 1)]
    per_token = (chosen[0].astype(F32) + chosen[1].astype(F32)).astype(BF)
    before = (
        lax.broadcasted_iota(jnp.int32, (rows, rows), 0) < lax.broadcasted_iota(jnp.int32, (rows, rows), 1)
    ).astype(F32).astype(BF)
    earlier = dot(per_token, before, ((1,), (0,)))
    numbers = lax.broadcasted_iota(jnp.int32, (count, rows), 0).astype(F32)
    for k in (0, 1):
        position = jnp.sum(jnp.where(chosen[k], earlier, 0.0), axis=0, keepdims=True)
        slot = ids[k : k + 1, :].astype(F32) * float(cap) + position
        hot[k] = (numbers == slot).astype(F32).astype(BF)

    for load in loads[2:8]:
        load.wait()
    for load in loads[8:]:
        load.start()
    own_rows = pl.ds(pl.multiple_of(z * cap, cap), cap)
    either = hot[0] + hot[1]
    for k in (0, 1):
        weights[k] = jnp.broadcast_to(weight[k : k + 1, :], (LANES, rows)).T

    def exchange(p, e):
        if p == 0:
            send[p, e] = dot(either, tok[e], ((1,), (0,))).astype(BF)
        else:
            wide = cot[e].astype(F32)
            send[p, e] = sum(dot(hot[k], (weights[k] * wide).astype(BF), ((1,), (0,))) for k in (0, 1)).astype(BF)
        if p == 0 and e == 0:
            pl.semaphore_wait(barrier, len(peers))
        s = own_slice(p, *DIRECT[e])
        for j in sorted(range(1, experts), key=lambda j: -min(j, experts - j)):
            to = (z + j) % experts
            to_rows = pl.ds(pl.multiple_of(to * cap, cap), cap)
            put(
                send.at[p, e, to_rows], slots.at[p, s, own_rows],
                z_s.at[p, e, j - 1], z_r.at[p, e, j - 1], device(z_=to),
            )
        slots[p, s, own_rows, :] = send[p, e, own_rows, :]

    for e in range(len(DIRECT)):
        for p in (0, 1):
            exchange(p, e)
    acc[...] = jnp.zeros_like(acc)
    pad = w_d.shape[0] - units
    if pad:
        w_d[pl.ds(units, pad), :] = jnp.zeros((pad, w_d.shape[1]), BF)
        hid_t[pl.ds(units, pad), :] = jnp.zeros((pad, count), BF)
    for k in (0, 1):
        hot_t[k] = hot[k].astype(F32).T.astype(BF)
    for load in loads[8:]:
        load.wait()

    def await_tokens(p, e):
        for j in range(1, experts):
            source = (z + experts - j) % experts
            from_rows = pl.ds(pl.multiple_of(source * cap, cap), cap)
            arrived(slots.at[p, own_slice(p, *DIRECT[e]), from_rows], z_s.at[p, e, j - 1], z_r.at[p, e, j - 1])

    def along(p, stage, step):
        return device(x_=at(x, step)) if (p == 0) == (stage == 0) else device(y_=at(y, step))

    def whole(p, s):
        return slots.at[p, s]

    def part_of(p, s, h):
        return slots.at[p, s, pl.ds(h * two, two)]

    def both_ways(p, stage, s, s_sem, r_sem):
        for n, step in ((0, LEFT), (1, RIGHT)):
            put(whole(p, s), whole(p, s), s_sem(n), r_sem(n), along(p, stage, step))

    def onward(p, stage, s, step, s_sem, r_sem):
        n, h, to = (3, 0, RIGHT) if step == LEFT else (2, 1, LEFT)
        ref = part_of(p, s, h)
        put(ref, ref, s_sem(n), r_sem(n), along(p, stage, to))

    def sem_a(p):
        return (lambda n: a_s.at[p, n]), (lambda n: a_r.at[p, n])

    def sem_b(p, k):
        return (lambda n: b_s.at[p, k, n]), (lambda n: b_r.at[p, k, n])

    def await_slice(p, k, m):
        if (k, m) in DIRECT:
            await_tokens(p, DIRECT.index((k, m)))
            return
        s = own_slice(p, k, m)
        step, (s_sem, r_sem) = (k, sem_a(p)) if m == 0 else (m, sem_b(p, k))
        if step == LEFT:
            arrived(whole(p, s), s_sem(1), r_sem(1))
        elif step == RIGHT:
            arrived(whole(p, s), s_sem(0), r_sem(0))
        else:
            arrived(part_of(p, s, 0), s_sem(3), r_sem(3))
            arrived(part_of(p, s, 1), s_sem(2), r_sem(2))

    def accumulate(p, k, m):
        x_, y_ = place(p, k, m)
        pair = [slice_of(x_, y_, e) for e in (0, 1)]
        cols = [pl.ds(pl.multiple_of(s * LANES, LANES), LANES) for s in pair]
        right = jnp.concatenate([slots[p, s] for s in pair], axis=1)
        if p == 0:
            left = jnp.concatenate([w_gu[:, d] for d in cols], axis=1)
            acc[pl.ds(0, 2 * units), :] += dot(left, right, ((1,), (1,)))
        else:
            left = jnp.concatenate([w_d[pl.ds(0, units), d] for d in cols], axis=1)
            acc[pl.ds(2 * units, units), :] += dot(left, right, ((1,), (1,)))

    def finish(event, parts=(0, 1)):
        for k, m in event:
            for p in parts:
                x_, y_ = place(p, k, m)
                arrived(whole(p, slice_of(x_, y_, 1 - c)), d_s.at[p, k, m], d_r.at[p, k, m])
        for k, m in event:
            for p in parts:
                accumulate(p, k, m)

    def take(p, k, m):
        await_slice(p, k, m)
        s = own_slice(p, k, m)
        if m == 0:
            if k == 0:
                both_ways(p, 0, s, *sem_a(p))
        elif m != FAR and k != FAR:
            onward(p, 1, s, m, *sem_b(p, k))

    def pass_on(p, k, m):
        s = own_slice(p, k, m)
        if m == 0:
            both_ways(p, 1, s, *sem_b(p, k))
        put(whole(p, s), whole(p, s), d_s.at[p, k, m], d_r.at[p, k, m], device(c_=1 - c))

    for p in (0, 1):
        take(p, 0, 0)
        pass_on(p, 0, 0)
    previous = EVENTS[0]
    for event in EVENTS[1:]:
        for k, m in event:
            for p in (0, 1):
                take(p, k, m)
        for k, m in event:
            for p in (0, 1):
                pass_on(p, k, m)
        finish(previous)
        previous = event
    finish(previous, (0,))

    block = BLOCK

    def activate(i, carry):
        r = pl.multiple_of(i * block, block)
        gate = acc[pl.ds(r, block), :]
        up = acc[pl.ds(units + r, block), :]
        s = jax.nn.sigmoid(gate)
        active = gate * s
        hid_t[pl.ds(r, block), :] = (active * up).astype(BF)
        acc[pl.ds(r, block), :] = up * (s * (1.0 + gate * (1.0 - s)))
        acc[pl.ds(units + r, block), :] = active
        return carry

    lax.fori_loop(0, units // block, activate, 0)
    for i in range(hid_t.shape[0] // LANES):
        r = pl.ds(i * LANES, LANES)
        hid[:, r] = hid_t[r, :].astype(F32).T.astype(BF)

    width = RING * LANES

    def terms(y_, c_):
        cols = pl.ds(pl.multiple_of((2 * y_ + c_) * width, width), width)
        return dot(hid[...], w_d[:, cols], ((1,), (0,)))

    for i in range(RING):
        t = terms(i, 1 - c)
        for n in range(RING):
            psend[i, n] = t[:, n * LANES : (n + 1) * LANES].astype(BF)
        put(psend.at[i], prem.at[i], p_s.at[i], p_r.at[i], device(c_=1 - c))
    for i in range(RING):
        t = terms(i, c)
        arrived(prem.at[i], p_s.at[i], p_r.at[i])
        for n in range(RING):
            part[i, n] = (t[:, n * LANES : (n + 1) * LANES] + prem[i, n].astype(F32)).astype(BF)

    def view(h, t, start, size):
        r = pl.ds(h * two + start, size)
        return (slice(None), t, r, slice(None)) if h == 0 else (t, slice(None), r, slice(None))

    first = [x, y]
    second = [y, x]

    def hop(h, stage, step):
        return device(x_=at(x, step)) if (h == 0) == (stage == 0) else device(y_=at(y, step))

    group, piece = two // 2, two // 4

    def term(h, t, r, n):
        return part.at[view(h, t, r * group + n * piece, piece)]

    def box(ref, h, side, r, n):
        return ref.at[h, side, :, pl.ds(r * group + n * piece, piece)]

    for r in (0, 1):
        for h in (0, 1):
            for n, step in ((0, RIGHT), (1, LEFT)):
                put(
                    term(h, at(first[h], FAR), r, n), relay.at[h, r, n],
                    q_s.at[h, r, n], q_r.at[h, r, n], hop(h, 0, step),
                )
        for h in (0, 1):
            for n, step in ((0, RIGHT), (1, LEFT)):
                put(
                    term(h, at(first[h], step), r, 1 - n), box(joined, h, n, r, 1 - n),
                    j_s.at[h, r, n, 0], j_r.at[h, r, n, 0], hop(h, 0, step),
                )
    finish(EVENTS[-1], (1,))

    def deltas(i, carry):
        r = pl.multiple_of(i * block, block)
        grad = acc[pl.ds(2 * units + r, block), :]
        delta[pl.ds(r, block), :] = (grad * acc[pl.ds(r, block), :]).astype(BF)
        delta[pl.ds(units + r, block), :] = (grad * acc[pl.ds(units + r, block), :]).astype(BF)
        return carry

    lax.fori_loop(0, units // block, deltas, 0)

    def gradients(i, squares):
        pair = [2 * i, 2 * i + 1]
        cols = pl.ds(pl.multiple_of(i * 2 * LANES, 2 * LANES), 2 * LANES)
        xs = jnp.concatenate([slots[0, s] for s in pair], axis=1)
        gs = jnp.concatenate([slots[1, s] for s in pair], axis=1)
        g = dot(delta[...], xs, ((1,), (0,)))
        grads[pl.ds(0, 2 * units), cols] = g
        squares += jnp.sum((g * g).reshape(2 * units // 8, 8, 2 * LANES), axis=0)
        g = dot(hid_t[pl.ds(0, units), :], gs, ((1,), (0,)))
        grads[pl.ds(2 * units, units), cols] = g
        return squares + jnp.sum((g * g).reshape(units // 8, 8, 2 * LANES), axis=0)

    def pass_terms(r):
        for h in (0, 1):
            for n, step in ((0, RIGHT), (1, LEFT)):
                arrived(relay.at[h, r, n], q_s.at[h, r, n], q_r.at[h, r, n])
                ref = term(h, at(first[h], step), r, n)
                ref[...] = (ref[...].astype(F32) + relay[h, r, n].astype(F32)).astype(BF)
                put(ref, box(joined, h, n, r, n), j_s.at[h, r, n, 1], j_r.at[h, r, n, 1], hop(h, 0, step))

    def across(r):
        for h in (0, 1):
            for n in (0, 1):
                arrived(box(joined, h, n, r, 1 - n), j_s.at[h, r, n, 0], j_r.at[h, r, n, 0])
                arrived(box(joined, h, n, r, n), j_s.at[h, r, n, 1], j_r.at[h, r, n, 1])
            v = pl.ds(r * group, group)
            half[h, :, v, :] = (
                part[view(h, first[h], r * group, group)].astype(F32)
                + joined[h, 0, :, v, :].astype(F32) + joined[h, 1, :, v, :].astype(F32)
            ).astype(BF)
            for j in (1, 2, 3):
                put(
                    half.at[h, at(second[h], j), v], last.at[h, j - 1, v],
                    l_s.at[h, r, j - 1], l_r.at[h, r, j - 1], hop(h, 1, j),
                )

    blocks = experts // 4
    place_of = (z % (2 * blocks)) // blocks * 2 * blocks + z // (2 * blocks) * blocks + z % blocks

    def give_back(r):
        for h in (0, 1):
            v = pl.ds(r * group, group)
            summed = half[h, second[h], v, :].astype(F32)
            for j in (1, 2, 3):
                arrived(last.at[h, j - 1, v], l_s.at[h, r, j - 1], l_r.at[h, r, j - 1])
                summed = summed + last[h, j - 1, v, :].astype(F32)
            final[pl.ds(h * two + r * group, group), :] = summed.astype(BF)
        for n in range(2 * blocks - 1) if r == 0 else range(2 * blocks - 1, experts - 1):
            i = n + jnp.where(n >= place_of, 1, 0)
            to = (i // blocks) % 2 * 2 * blocks + i // (2 * blocks) * blocks + i % blocks
            to_rows = pl.ds(pl.multiple_of(to * cap, cap), cap)
            put(final.at[to_rows], back.at[own_rows], k_s.at[n], k_r.at[z], device(z_=to))

    def share(stage, value, devices, base):
        sq_send[stage] = value
        for n, dev in enumerate(devices):
            put(sq_send.at[stage], sq_recv.at[base + n], sq_s.at[base + n], sq_r.at[base + n], dev)

    def gathered(value, base, n):
        for i in range(base, base + n):
            arrived(sq_recv.at[i], sq_s.at[i], sq_r.at[i])
            value = value + sq_recv[i]
        return value

    pairs = slots.shape[1] // 2
    squares = lax.fori_loop(0, pairs // 2, gradients, jnp.zeros((8, 2 * LANES), F32))
    pass_terms(0)
    squares = lax.fori_loop(pairs // 2, pairs, gradients, squares)
    value = squares[:, :LANES] + squares[:, LANES:]
    share(0, value, [device(c_=1 - c)], 0)
    value = gathered(value, 0, 1)
    share(1, value, [device(x_=at(x, s)) for s in (1, 2, 3)], 1)
    pass_terms(1)
    across(0)
    value = gathered(value, 1, 3)
    share(2, value, [device(y_=at(y, s)) for s in (1, 2, 3)], 4)
    across(1)
    value = gathered(value, 4, 3)
    share(3, value, [device(z_=(z + j) % experts) for j in range(1, experts)], 7)
    give_back(0)
    give_back(1)
    back[own_rows, :] = final[own_rows, :]
    value = gathered(value, 7, experts - 1)
    inv = lax.rsqrt(jnp.sum(value, keepdims=True) / total + 1e-06)

    def scale(i, carry):
        r = pl.ds(pl.multiple_of(i * block, block), block)
        scaled_out[r, :] = (grads[r, :] * inv).astype(BF)
        return carry

    lax.fori_loop(0, 3 * units // block, scale, 0)
    for j in range(1, experts):
        source = (z + experts - j) % experts
        from_rows = pl.ds(pl.multiple_of(source * cap, cap), cap)
        arrived(back.at[from_rows], k_s.at[0], k_r.at[source])
    picked = [dot(hot_t[k], back[...], ((1,), (0,))) for k in (0, 1)]
    layer_out[...] = (weights[0] * picked[0] + weights[1] * picked[1]).astype(BF)
    for copy in started:
        copy.wait_send()


def copy_body(scaled, layer, gate_out, up_out, down_out, layer_out, sems):
    units = gate_out.shape[0]
    copies = [
        pltpu.make_async_copy(scaled.at[pl.ds(n * units, units)], out, sems.at[n])
        for n, out in enumerate((gate_out, up_out, down_out))
    ]
    for copy in copies:
        copy.start()
    layer_out[...] = layer[...]
    for copy in copies:
        copy.wait()


def solution(mesh):
    experts = mesh.shape["expert"]
    groups = mesh.shape["dp"] * mesh.shape["ffn"]

    def on_device(tokens, expert_ids, route_weight, cotangent, w_gate, w_up, w_down):
        rows, features = tokens.shape
        units = w_gate.shape[1]
        padded = -(-units // LANES) * LANES
        count = experts * rows // 2
        two, four = count // 2, count // 4
        total = 3.0 * experts * units * groups * features
        vmem, anywhere = pl.BlockSpec(memory_space=pltpu.VMEM), pl.BlockSpec(memory_space=pltpu.HBM)
        dma = pltpu.SemaphoreType.DMA
        scaled, layer = pl.pallas_call(
            functools.partial(body, experts=experts, total=total),
            out_shape=[
                jax.ShapeDtypeStruct((3 * units, features), BF),
                jax.ShapeDtypeStruct((rows, LANES), BF),
            ],
            in_specs=[anywhere] * 7,
            out_specs=[vmem] * 2,
            scratch_shapes=[
                pltpu.VMEM((2, rows), jnp.int32),
                pltpu.VMEM((2, rows), F32),
                pltpu.VMEM((3 * units, features), F32),
                pltpu.VMEM((len(DIRECT), rows, LANES), BF),
                pltpu.VMEM((len(DIRECT), rows, LANES), BF),
                pltpu.VMEM((2, count, rows), BF),
                pltpu.VMEM((2, rows, count), BF),
                pltpu.VMEM((2, len(DIRECT), count, LANES), BF),
                pltpu.VMEM((2, groups, count, LANES), BF),
                pltpu.VMEM((2 * units, features), BF),
                pltpu.VMEM((padded, features), BF),
                pltpu.VMEM((3 * units, count), F32),
                pltpu.VMEM((padded, count), BF),
                pltpu.VMEM((count, padded), BF),
                pltpu.VMEM((2 * units, count), BF),
                pltpu.VMEM((2, rows, LANES), F32),
                pltpu.VMEM((RING, RING, count, LANES), BF),
                pltpu.VMEM((RING, RING, count, LANES), BF),
                pltpu.VMEM((RING, RING, count, LANES), BF),
                pltpu.VMEM((2, 2, 2, RING, four // 2, LANES), BF),
                pltpu.VMEM((2, 2, RING, two, LANES), BF),
                pltpu.VMEM((2, RING, two, LANES), BF),
                pltpu.VMEM((2, 3, two, LANES), BF),
                pltpu.VMEM((count, LANES), BF),
                pltpu.VMEM((count, LANES), BF),
                pltpu.VMEM((4, 8, LANES), F32),
                pltpu.VMEM((6 + experts, 8, LANES), F32),
                dma((11,)),
                dma((2, len(DIRECT), experts - 1)), dma((2, len(DIRECT), experts - 1)),
                dma((2, 4)), dma((2, 4)),
                dma((2, RING, 4)), dma((2, RING, 4)),
                dma((2, RING, RING)), dma((2, RING, RING)),
                dma((RING,)), dma((RING,)),
                dma((2, 2, 2)), dma((2, 2, 2)),
                dma((2, 2, 2, 2)), dma((2, 2, 2, 2)),
                dma((2, 2, 3)), dma((2, 2, 3)),
                dma((experts - 1,)), dma((experts,)),
                dma((6 + experts,)), dma((6 + experts,)),
            ],
            compiler_params=pltpu.CompilerParams(
                collective_id=0, has_side_effects=True, vmem_limit_bytes=VMEM
            ),
            name="layer",
        )(
            *[
                pltpu.with_memory_space_constraint(a, pltpu.HBM)
                for a in (expert_ids.T, route_weight.T, tokens, cotangent, w_gate, w_up, w_down)
            ]
        )
        gate, up, down, layer = pl.pallas_call(
            copy_body,
            out_shape=[jax.ShapeDtypeStruct((units, features), BF)] * 3
            + [jax.ShapeDtypeStruct((rows, LANES), BF)],
            in_specs=[vmem] * 2,
            out_specs=[anywhere] * 3 + [vmem],
            scratch_shapes=[dma((3,))],
            compiler_params=pltpu.CompilerParams(vmem_limit_bytes=COPY_VMEM),
            name="copy_out",
        )(scaled, layer)
        return layer, gate[None], up[None], down[None]

    token, hidden = P("expert", None), P("expert", ("dp", "ffn"), None)
    return jax.shard_map(
        on_device,
        mesh=mesh,
        in_specs=(token, token, token, token, hidden, hidden, hidden),
        out_specs=(P("expert", ("dp", "ffn")), hidden, hidden, hidden),
        check_vma=False,
    )
```

time: 79.1 us -> 71.1 us (0.90); the launches traced: 79 us -> 70.2 us
  Pallas kernels: 77 us -> 69.5 us
  local copies, waits for them, and re-layouts: 1.35 us -> 0 us
    pallas_call x1, Pallas kernels: 73.7 us -> 66.4 us  [on_device(): pl.pallas_call(functools.partial(body, experts=experts, total=total), out...]
    unnamed x4 -> x0, local copies, waits for them, and re-layouts: 1.35 us -> none
where the time goes in v4:
time: 71.1 us; the launch traced here: 70.2 us
  Pallas kernels  69.5 us (98%)
    pallas_call x1, Pallas kernels, on_device(): pl.pallas_call(functools.partial(body, experts=experts, total=total), out...  66.4 us
    pallas_call x1, Pallas kernels, on_device(): pl.pallas_call(copy_body, out_shape=[jax.ShapeDtypeStruct((units, feature...  3.08 us

profile of v4, /device:TPU:2, one launch (start us, length us, event | category | flops | bytes accessed | tf_op | source)
XLA Modules:
  0.0 70.2 jit_solution(1626812733131793703)
XLA Ops:
  0.6 66.4 %layer.1 = (bf16[672,4096]{1,0:T(8,128)(2,1)S(1)}, bf16[128,128]{1,0:T(8,128)(2,1)S(1)}) custom-call(s32[2,128]{1,0:T(2,128)} %bitcast.5, f32[2,128]{1,0:T(2,128)} %bitcast.6, bf16[128,4096]{1,0:T(8,128)(2,1)} %tokens.1, bf16[128,4096]{1,0:T(8,128)(2,1)} %cotangent.1, bf16[1,224,4096]{2,1,0:T(8,128)(2,1)} %w_gate.1, bf16[1,224,4096]{2,1,0:T(8,128)(2,1)} %w_up.1, ...), custom_call_target="tpu_custom_call" | custom-call | tf_op jit(solution)/shard_map/layer/pallas_call | solution.py:462
  67.1 3.1 %copy_out.1 = (bf16[224,4096]{1,0:T(8,128)(2,1)}, bf16[224,4096]{1,0:T(8,128)(2,1)}, bf16[224,4096]{1,0:T(8,128)(2,1)}, bf16[128,128]{1,0:T(8,128)(2,1)}) custom-call(bf16[672,4096]{1,0:T(8,128)(2,1)S(1)} %get-tuple-element.10.scaled, bf16[128,128]{1,0:T(8,128)(2,1)S(1)} %get-tuple-element.11.layer), custom_call_target="tpu_custom_call" | custom-call | tf_op jit(solution)/shard_map/copy_out/pallas_call | solution.py:520

commit v5 on v4

--- a/solution.py
+++ b/solution.py
@@ -22,9 +22,9 @@
     ((0, LEFT), (0, RIGHT)),
     ((FAR, 0),),
     ((LEFT, LEFT), (LEFT, RIGHT), (RIGHT, LEFT), (RIGHT, RIGHT)),
-    ((0, FAR),),
+    ((0, FAR), (FAR, FAR)),
     ((FAR, LEFT), (FAR, RIGHT)),
-    ((FAR, FAR), (LEFT, FAR), (RIGHT, FAR)),
+    ((LEFT, FAR), (RIGHT, FAR)),
 )
 DIRECT = ((0, 0), (FAR, 0), (FAR, FAR))
 
@@ -35,9 +35,9 @@
 
 def body(
     ids_in, weight_in, tokens, cotangent, w_gate, w_up, w_down,
-    scaled_out, layer_out,
-    ids, weight, grads, tok, cot, hot, hot_t, send, slots, w_gu, w_d, acc, hid_t, hid, delta, weights,
-    psend, prem, part, relay, joined, half, last, final, back, sq_send, sq_recv,
+    scaled_out, back, hot_t, weights,
+    ids, weight, grads, tok, cot, hot, send, slots, w_gu, w_d, acc, hid_t, hid, delta,
+    psend, prem, part, relay, joined, half, last, final, sq_send, sq_recv,
     local, z_s, z_r, a_s, a_r, b_s, b_r, d_s, d_r, p_s, p_r, q_s, q_r, j_s, j_r,
     l_s, l_r, k_s, k_r, sq_s, sq_r,
     *, experts, total,
@@ -397,9 +397,9 @@
         return value
 
     pairs = slots.shape[1] // 2
-    squares = lax.fori_loop(0, pairs // 2, gradients, jnp.zeros((8, 2 * LANES), F32))
+    squares = lax.fori_loop(0, 3 * pairs // 4, gradients, jnp.zeros((8, 2 * LANES), F32))
     pass_terms(0)
-    squares = lax.fori_loop(pairs // 2, pairs, gradients, squares)
+    squares = lax.fori_loop(3 * pairs // 4, pairs, gradients, squares)
     value = squares[:, :LANES] + squares[:, LANES:]
     share(0, value, [device(c_=1 - c)], 0)
     value = gathered(value, 0, 1)
@@ -423,25 +423,27 @@
         return carry
 
     lax.fori_loop(0, 3 * units // block, scale, 0)
+    for copy in started:
+        copy.wait_send()
     for j in range(1, experts):
         source = (z + experts - j) % experts
         from_rows = pl.ds(pl.multiple_of(source * cap, cap), cap)
         arrived(back.at[from_rows], k_s.at[0], k_r.at[source])
-    picked = [dot(hot_t[k], back[...], ((1,), (0,))) for k in (0, 1)]
-    layer_out[...] = (weights[0] * picked[0] + weights[1] * picked[1]).astype(BF)
-    for copy in started:
-        copy.wait_send()
-
-
-def copy_body(scaled, layer, gate_out, up_out, down_out, layer_out, sems):
+
+
+def copy_body(scaled, back, hot_t, weights, gate_out, up_out, down_out, layer_out, sems):
     units = gate_out.shape[0]
+    blocks = units // BLOCK
     copies = [
-        pltpu.make_async_copy(scaled.at[pl.ds(n * units, units)], out, sems.at[n])
-        for n, out in enumerate((gate_out, up_out, down_out))
+        pltpu.make_async_copy(
+            scaled.at[pl.ds(n * units + i * BLOCK, BLOCK)], out.at[pl.ds(i * BLOCK, BLOCK)], sems.at[n * blocks + i]
+        )
+        for i in range(blocks) for n, out in enumerate((gate_out, up_out, down_out))
     ]
     for copy in copies:
         copy.start()
-    layer_out[...] = layer[...]
+    picked = [dot(hot_t[k], back[...], ((1,), (0,))) for k in (0, 1)]
+    layer_out[...] = (weights[0] * picked[0] + weights[1] * picked[1]).astype(BF)
     for copy in copies:
         copy.wait()
 
@@ -459,14 +461,16 @@
         total = 3.0 * experts * units * groups * features
         vmem, anywhere = pl.BlockSpec(memory_space=pltpu.VMEM), pl.BlockSpec(memory_space=pltpu.HBM)
         dma = pltpu.SemaphoreType.DMA
-        scaled, layer = pl.pallas_call(
+        scaled, back, hot_t, weights = pl.pallas_call(
             functools.partial(body, experts=experts, total=total),
             out_shape=[
                 jax.ShapeDtypeStruct((3 * units, features), BF),
-                jax.ShapeDtypeStruct((rows, LANES), BF),
+                jax.ShapeDtypeStruct((count, LANES), BF),
+                jax.ShapeDtypeStruct((2, rows, count), BF),
+                jax.ShapeDtypeStruct((2, rows, LANES), F32),
             ],
             in_specs=[anywhere] * 7,
-            out_specs=[vmem] * 2,
+            out_specs=[vmem] * 4,
             scratch_shapes=[
                 pltpu.VMEM((2, rows), jnp.int32),
                 pltpu.VMEM((2, rows), F32),
@@ -474,7 +478,6 @@
                 pltpu.VMEM((len(DIRECT), rows, LANES), BF),
                 pltpu.VMEM((len(DIRECT), rows, LANES), BF),
                 pltpu.VMEM((2, count, rows), BF),
-                pltpu.VMEM((2, rows, count), BF),
                 pltpu.VMEM((2, len(DIRECT), count, LANES), BF),
                 pltpu.VMEM((2, groups, count, LANES), BF),
                 pltpu.VMEM((2 * units, features), BF),
@@ -483,7 +486,6 @@
                 pltpu.VMEM((padded, count), BF),
                 pltpu.VMEM((count, padded), BF),
                 pltpu.VMEM((2 * units, count), BF),
-                pltpu.VMEM((2, rows, LANES), F32),
                 pltpu.VMEM((RING, RING, count, LANES), BF),
                 pltpu.VMEM((RING, RING, count, LANES), BF),
                 pltpu.VMEM((RING, RING, count, LANES), BF),
@@ -491,7 +493,6 @@
                 pltpu.VMEM((2, 2, RING, two, LANES), BF),
                 pltpu.VMEM((2, RING, two, LANES), BF),
                 pltpu.VMEM((2, 3, two, LANES), BF),
-                pltpu.VMEM((count, LANES), BF),
                 pltpu.VMEM((count, LANES), BF),
                 pltpu.VMEM((4, 8, LANES), F32),
                 pltpu.VMEM((6 + experts, 8, LANES), F32),
@@ -521,12 +522,12 @@
             copy_body,
             out_shape=[jax.ShapeDtypeStruct((units, features), BF)] * 3
             + [jax.ShapeDtypeStruct((rows, LANES), BF)],
-            in_specs=[vmem] * 2,
+            in_specs=[vmem] * 4,
             out_specs=[anywhere] * 3 + [vmem],
-            scratch_shapes=[dma((3,))],
+            scratch_shapes=[dma((3 * (units // BLOCK),))],
             compiler_params=pltpu.CompilerParams(vmem_limit_bytes=COPY_VMEM),
             name="copy_out",
-        )(scaled, layer)
+        )(scaled, back, hot_t, weights)
         return layer, gate[None], up[None], down[None]
 
     token, hidden = P("expert", None), P("expert", ("dp", "ffn"), None)

time: 71.1 us -> 70 us (0.985)
  Pallas kernels: 69.5 us -> 68.4 us
    pallas_call x1, Pallas kernels: 66.4 us -> 65.2 us  [on_device(): pl.pallas_call(functools.partial(body, experts=experts, total=total), out...]
where the time goes in v5:
time: 70 us; the launch traced here: 69.1 us
  Pallas kernels  68.4 us (98%)
    pallas_call x1, Pallas kernels, on_device(): pl.pallas_call(functools.partial(body, experts=experts, total=total), out...  65.2 us
    pallas_call x1, Pallas kernels, on_device(): pl.pallas_call(copy_body, out_shape=[jax.ShapeDtypeStruct((units, feature...  3.25 us

profile of v5, /device:TPU:2, one launch (start us, length us, event | category | flops | bytes accessed | tf_op | source)
XLA Modules:
  0.0 69.1 jit_solution(3429927331666534851)
XLA Ops:
  0.6 65.2 %layer.1 = (bf16[672,4096]{1,0:T(8,128)(2,1)S(1)}, bf16[512,128]{1,0:T(8,128)(2,1)S(1)}, bf16[2,128,512]{2,1,0:T(8,128)(2,1)S(1)}, f32[2,128,128]{2,1,0:T(8,128)S(1)}) custom-call(s32[2,128]{1,0:T(2,128)} %bitcast.5, f32[2,128]{1,0:T(2,128)} %bitcast.6, bf16[128,4096]{1,0:T(8,128)(2,1)} %tokens.1, bf16[128,4096]{1,0:T(8,128)(2,1)} %cotangent.1, ...), custom_call_target="tpu_custom_call" | custom-call | tf_op jit(solution)/shard_map/layer/pallas_call | solution.py:464
  65.8 3.2 %copy_out.1 = (bf16[224,4096]{1,0:T(8,128)(2,1)}, bf16[224,4096]{1,0:T(8,128)(2,1)}, bf16[224,4096]{1,0:T(8,128)(2,1)}, bf16[128,128]{1,0:T(8,128)(2,1)}) custom-call(bf16[672,4096]{1,0:T(8,128)(2,1)S(1)} %get-tuple-element.12.scaled, bf16[512,128]{1,0:T(8,128)(2,1)S(1)} %get-tuple-element.13.back, bf16[2,128,512]{2,1,0:T(8,128)(2,1)S(1)} %get-tuple-element.14.hot_t, ...), custom_call_target="tpu_custom_call" | custom-call | tf_op jit(solution)/shard_map/copy_out/pallas_call | solution.py:521

commit v6 on v5

--- a/solution.py
+++ b/solution.py
@@ -120,14 +120,9 @@
         slot = ids[k : k + 1, :].astype(F32) * float(cap) + position
         hot[k] = (numbers == slot).astype(F32).astype(BF)
 
-    for load in loads[2:8]:
-        load.wait()
-    for load in loads[8:]:
-        load.start()
+    loads[2].wait()
     own_rows = pl.ds(pl.multiple_of(z * cap, cap), cap)
     either = hot[0] + hot[1]
-    for k in (0, 1):
-        weights[k] = jnp.broadcast_to(weight[k : k + 1, :], (LANES, rows)).T
 
     def exchange(p, e):
         if p == 0:
@@ -147,9 +142,17 @@
             )
         slots[p, s, own_rows, :] = send[p, e, own_rows, :]
 
+    exchange(0, 0)
+    for load in loads[3:8]:
+        load.wait()
+    for load in loads[8:]:
+        load.start()
+    for k in (0, 1):
+        weights[k] = jnp.broadcast_to(weight[k : k + 1, :], (LANES, rows)).T
     for e in range(len(DIRECT)):
         for p in (0, 1):
-            exchange(p, e)
+            if (p, e) != (0, 0):
+                exchange(p, e)
     acc[...] = jnp.zeros_like(acc)
     pad = w_d.shape[0] - units
     if pad:

time: 70 us -> 70 us (level)
  no operation moved by 1% of the time
where the time goes in v6:
time: 70 us; the launch traced here: 69.1 us
  Pallas kernels  68.4 us (98%)
    pallas_call x1, Pallas kernels, on_device(): pl.pallas_call(functools.partial(body, experts=experts, total=total), out...  65.2 us
    pallas_call x1, Pallas kernels, on_device(): pl.pallas_call(copy_body, out_shape=[jax.ShapeDtypeStruct((units, feature...  3.25 us

profile of v6, /device:TPU:2, one launch (start us, length us, event | category | flops | bytes accessed | tf_op | source)
XLA Modules:
  0.0 69.1 jit_solution(2878219649079043713)
XLA Ops:
  0.6 65.2 %layer.1 = (bf16[672,4096]{1,0:T(8,128)(2,1)S(1)}, bf16[512,128]{1,0:T(8,128)(2,1)S(1)}, bf16[2,128,512]{2,1,0:T(8,128)(2,1)S(1)}, f32[2,128,128]{2,1,0:T(8,128)S(1)}) custom-call(s32[2,128]{1,0:T(2,128)} %bitcast.5, f32[2,128]{1,0:T(2,128)} %bitcast.6, bf16[128,4096]{1,0:T(8,128)(2,1)} %tokens.1, bf16[128,4096]{1,0:T(8,128)(2,1)} %cotangent.1, ...), custom_call_target="tpu_custom_call" | custom-call | tf_op jit(solution)/shard_map/layer/pallas_call | solution.py:467
  65.8 3.2 %copy_out.1 = (bf16[224,4096]{1,0:T(8,128)(2,1)}, bf16[224,4096]{1,0:T(8,128)(2,1)}, bf16[224,4096]{1,0:T(8,128)(2,1)}, bf16[128,128]{1,0:T(8,128)(2,1)}) custom-call(bf16[672,4096]{1,0:T(8,128)(2,1)S(1)} %get-tuple-element.12.scaled, bf16[512,128]{1,0:T(8,128)(2,1)S(1)} %get-tuple-element.13.back, bf16[2,128,512]{2,1,0:T(8,128)(2,1)S(1)} %get-tuple-element.14.hot_t, ...), custom_call_target="tpu_custom_call" | custom-call | tf_op jit(solution)/shard_map/copy_out/pallas_call | solution.py:524
